TPU v7x, 32 devices: a whole 2x2x4 slice. The times are simulated.
32 devices in a mesh: lat: 16 (over z, y, x), fld: 2 (over core).
Axes of the slice: x: 2, y: 2, z: 4, core: 2. Of those that a mesh axis runs over, the one named last changes fastest.
Arguments:
- grid: bfloat16 [2, 4, 69, 640, 1408], P('fld', None, None, 'lat'), may hold values from -6 to 6
- cycle_ids: int32 [640], replicated, may hold values from 0 to 639, each once
- cycle_len: int32 [640], replicated, may hold values from 20 to 1296, as said below
- wave_ids: int32 [320], replicated, may hold values from 0 to 319, each once
- legendre: bfloat16 [320, 320, 640], P('lat'), may hold values from -0.25 to 0.25
- target: float32 [2, 4, 69, 2, 320, 320], P('fld', None, None, None, 'lat'), may hold values from -18 to 18
- step_w: float32 [2], P('fld'), may hold values from 0.5 to 2
- chan_w: float32 [69], replicated, may hold values from 0.2 to 2
Outputs:
- coeffs: float32 [2, 4, 69, 2, 320, 320], P('fld', None, None, None, 'lat')
- loss: float32 [], replicated
- field_grad: bfloat16 [2, 4, 69, 640, 1408], P('fld', None, None, 'lat')
Inputs may be any that keep to these rules, and one draw needn't show every extreme that they name: `cycle_len`: every length 20 + 4 j with j from 0 to 319 occurs exactly twice.
All inputs are finite; a program needn't handle non-finite values.
Results may differ from a plain program's by a relative error of at most 0.0065.
Values may be sent and summed in bfloat16 or wider, within the bound.
No kernel may reach another device: no remote copies, remote signals or barrier semaphores. Data moves between devices by JAX's collectives and lax.ppermute only.
A program may use at most 320 MiB of HBM per device.

v0:
```python
import math

import jax
import jax.numpy as jnp
from jax import lax
from jax.sharding import PartitionSpec as P

STEPS = 2


def cycle_table(length, wave_order, segment):
    slot_index = jnp.arange(segment, dtype=jnp.int32)
    phase_int = slot_index[:, None] * wave_order[None, :] % length
    angles = 2.0 * math.pi / length.astype(jnp.float32) * phase_int.astype(jnp.float32)
    inside = (slot_index[:, None] < length) & (2 * wave_order[None, :] < length)
    row_scale = jnp.where(inside, lax.rsqrt(length.astype(jnp.float32)), jnp.float32(0.0))
    paired = jnp.stack([jnp.cos(angles) * row_scale, -jnp.sin(angles) * row_scale], axis=2)
    return paired.reshape(segment, 2 * wave_order.shape[0]).astype(jnp.bfloat16)


def owner_pass(
    part_fourier, legendre_cols, kept_mask, factor, target_part, weight_part, send_out, send_back
):
    gathered = send_out(part_fourier)
    coeffs = jnp.einsum(
        "jnr,rbjp->jnbp", legendre_cols, gathered, preferred_element_type=jnp.float32
    )
    coeffs = coeffs * kept_mask
    weight = factor[:, None, None, None] * weight_part[None, None, :, None]
    misfit = (coeffs - target_part) * kept_mask
    partial_value = jnp.sum(weight * misfit * misfit)
    grad_coeff = (2.0 * weight * misfit).astype(jnp.bfloat16)
    back_rows = jnp.einsum(
        "jnr,jnbp->rbjp", legendre_cols, grad_coeff, preferred_element_type=jnp.float32
    )
    back_rows = back_rows.astype(jnp.bfloat16)
    returned = send_back(back_rows)
    return (coeffs, partial_value, returned)


def per_device(grid, cycle_ids, cycle_len, wave_ids, legendre, target, step_w, chan_w):
    batch_size, chan_count, cycle_dev, segment = (
        grid.shape[1],
        grid.shape[2],
        grid.shape[3],
        grid.shape[4],
    )
    wave_count = wave_ids.shape[0]
    wave_dev = legendre.shape[0]
    col_count = batch_size * chan_count
    lat_index = lax.axis_index("lat")
    my_cycles = lax.dynamic_slice_in_dim(cycle_ids, lat_index * cycle_dev, cycle_dev)
    lengths = jnp.take(cycle_len, my_cycles)
    tables = jax.vmap(lambda length: cycle_table(length, wave_ids, segment))(lengths)
    fourier = jnp.einsum("bcrk,rkj->rbcj", grid[0], tables, preferred_element_type=jnp.float32)
    fourier = fourier.astype(jnp.bfloat16).reshape(cycle_dev, col_count, wave_count, 2)
    my_waves = lax.dynamic_slice_in_dim(wave_ids, lat_index * wave_dev, wave_dev)
    legendre_cols = jnp.take(legendre, cycle_ids, axis=2)
    degree = jnp.arange(wave_count, dtype=jnp.int32)
    kept_mask = (degree[None, :] >= my_waves[:, None]).astype(jnp.float32)[:, :, None, None]
    target_local = jnp.transpose(
        target[0].reshape(col_count, 2, wave_dev, wave_count), (2, 3, 0, 1)
    )
    factor = jnp.where(my_waves == 0, 1.0, 2.0).astype(jnp.float32)
    weight_cols = jnp.broadcast_to(step_w[0] * chan_w[None, :], (batch_size, chan_count)).reshape(
        col_count
    )

    def send_out(values):
        return lax.all_to_all(values, "lat", split_axis=2, concat_axis=0, tiled=True)

    def send_back(values):
        return lax.all_to_all(values, "lat", split_axis=0, concat_axis=2, tiled=True)

    coeff_piece, partial_piece, returned_piece = owner_pass(
        fourier, legendre_cols, kept_mask, factor, target_local, weight_cols, send_out, send_back
    )
    returned = returned_piece
    returned = returned.reshape(cycle_dev, col_count, 2 * wave_count)
    field_rows = jnp.einsum("rbj,rkj->brk", returned, tables, preferred_element_type=jnp.float32)
    field_grad = field_rows.astype(jnp.bfloat16).reshape(
        1, batch_size, chan_count, cycle_dev, segment
    )
    coeff_out = jnp.transpose(coeff_piece, (2, 3, 0, 1)).reshape(
        1, batch_size, chan_count, 2, wave_dev, wave_count
    )
    loss_sum = lax.psum(partial_piece, ("lat", "fld"))
    term_count = STEPS * batch_size * chan_count * wave_count * (wave_count + 1) // 2
    loss = loss_sum / jnp.float32(term_count)
    return (coeff_out, loss, field_grad)


def solution(mesh):
    return jax.shard_map(
        per_device,
        mesh=mesh,
        in_specs=(
            P("fld", None, None, "lat", None),
            P(),
            P(),
            P(),
            P("lat", None, None),
            P("fld", None, None, None, "lat", None),
            P("fld"),
            P(),
        ),
        out_specs=(P("fld", None, None, None, "lat", None), P(), P("fld", None, None, "lat", None)),
        check_vma=False,
    )
```

profile of v0, /device:TPU:28, one launch (start us, length us, event | category | flops | bytes accessed | tf_op | source)
XLA Modules:
  0.0 2602.2 jit_solution(16800594429964141860)
XLA Ops:
  0.7 0.8 compare_select_fusion.2
  1.4 0.7 gather_fusion.1
  2.2 0.8 broadcast_compare_fusion.1
  2.9 0.1 iota_compare_fusion
  3.1 0.7 broadcast_multiply_fusion.2
  3.7 0.9 iota_multiply_fusion
  4.6 0.1 broadcast_compare_fusion
  4.7 1187.4 %fusion = (bf16[40,1408,320,1]{1,0,3,2:T(8,128)(2,1)}, bf16[40,1408,320,1]{1,0,3,2:T(8,128)(2,1)}) fusion(f32[40]{0:T(128)S(1)} %get-tuple-element.17, s32[40]{0:T(128)S(1)} %compare_select_fusion.1, s32[1408,320]{0,1:T(8,128)S(1)} %iota_multiply_fusion, f32[40]{0:T(128)S(1)} %get-tuple-element.16, pred[40]{0:T(512)(128)(4,1)S(1)} %get-tuple-element.8, ...), kind=kLoop, calls=%fused_computation.8 | loop fusion | flops 288358400 | bytes 73961480 | tf_op jit(solution)/shard_map/convert
  1192.1 48.1 %pad_maximum_fusion = bf16[40,1408,320,2]{1,0,3,2:T(8,128)(2,1)} fusion(bf16[40,1408,320,1]{1,0,3,2:T(8,128)(2,1)} %get-tuple-element.13, bf16[40,1408,320,1]{1,0,3,2:T(8,128)(2,1)} %get-tuple-element.12), kind=kLoop, calls=%fused_computation.15 | loop fusion | flops 36044800 | bytes 144179200 | tf_op jit(solution)/shard_map/vmap()/stack | solution.py:17
  1240.2 88.0 %convert_bitcast_fusion.1 = bf16[40,4,69,640]{3,2,1,0:T(8,128)(2,1)} fusion(bf16[4,69,40,1408]{3,2,1,0:T(8,128)(2,1)} %bitcast.51, bf16[40,1408,640,1]{1,0,2,3:T(8,128)(2,1)} %bitcast.3), kind=kOutput, calls=%fused_computation.31 | convolution fusion | flops 19903795200 | bytes 117309440 | tf_op jit(solution)/shard_map/bcrk,rkj->rbcj/dot_general | solution.py:55
  1328.2 41.0 %copy.35 = bf16[40,4,69,640]{2,1,0,3:T(4,128)(2,1)} copy(bf16[40,4,69,640]{3,2,1,0:T(8,128)(2,1)} %convert_bitcast_fusion.1) | data formatting | bytes 28262400 | tf_op jit(solution)/shard_map/convert_element_type | solution.py:56
  1369.2 40.3 %reshape.263 = bf16[40,276,320,2]{1,0,3,2:T(8,128)(2,1)} reshape(bf16[40,4,69,640]{2,1,0,3:T(4,128)(2,1)} %copy.35) | data formatting | bytes 28262400 | tf_op jit(solution)/shard_map/reshape | solution.py:56
  1409.6 7.3 all-to-all-start
  1416.9 15.0 copy.32
  1431.9 25.5 gather_fusion
  1457.4 11.0 select_bitcast_fusion
  1468.4 14.9 copy.49
  1484.0 0.1 mul.164
  1484.1 0.8 compare_select_fusion.3
  1485.0 381.0 %all-to-all-done = bf16[40,276,320,2]{1,0,3,2:T(8,128)(2,1)} async-done(((bf16[40,276,320,2]{1,0,3,2:T(8,128)(2,1)}), bf16[40,276,320,2]{1,0,3,2:T(8,128)(2,1)}, u32[]{:S(2)}, u32[]{:S(2)}) %all-to-all-start) | async-done | bytes 14131232 | tf_op jit(solution)/shard_map/all_to_all | solution.py:70
  1866.0 17.2 copy.36
  1883.3 18.7 fusion.26
  1901.9 23.3 convert_bitcast_fusion.2
  1925.3 47.3 %copy.42 = bf16[640,276,20,2]{1,3,2,0:T(2,128)(2,1)} copy(bf16[640,276,20,2]{0,1,3,2:T(8,128)(2,1)} %convert_bitcast_fusion.2) | data formatting | bytes 28262400 | tf_op jit(solution)/shard_map/convert_element_type | solution.py:36
  1972.6 6.0 all-to-all-start.1
  1978.6 18.9 fusion.17
  1997.5 446.2 %psum.7 = f32[]{:T(128)} all-reduce(f32[]{:T(128)} %get-tuple-element.10), channel_id=1, replica_groups=mesh['lat'=16,'fld'=2] {'lat','fld'}, use_global_device_ids=true, to_apply=%region_1.2 | all-reduce | flops 1 | bytes 8 | tf_op jit(solution)/shard_map/psum | solution.py:87
  2443.8 30.0 %copy.39 = f32[276,2,20,320]{3,1,2,0:T(2,128)} copy(f32[276,2,20,320]{3,0,1,2:T(8,128)} %get-tuple-element.11) | data formatting | bytes 28262400 | tf_op jit(solution)/shard_map/mul | solution.py:28
  2474.4 11.8 copy.43
  2486.2 7.0 copy.44
  2493.3 72.0 %convert_bitcast_fusion = bf16[276,40,1408]{2,0,1:T(8,128)(2,1)} fusion(bf16[40,1408,640]{1,0,2:T(8,128)(2,1)} %bitcast.2, bf16[40,276,640]{1,0,2:T(8,128)(2,1)} %bitcast.49), kind=kOutput, calls=%fused_computation.23 | convolution fusion | flops 19912273920 | bytes 117309440 | tf_op jit(solution)/shard_map/rbj,rkj->brk/dot_general | solution.py:80
  2565.2 35.6 %copy.47 = bf16[276,40,1408]{2,1,0:T(8,128)(2,1)} copy(bf16[276,40,1408]{2,0,1:T(8,128)(2,1)} %convert_bitcast_fusion) | data formatting | bytes 62177280 | tf_op jit(solution)/shard_map/convert_element_type | solution.py:81
  (21 shorter events, 0.2 us)
Async XLA Ops:
  0.6 0.8 copy-start
  1409.6 456.4 %all-to-all-start = ((bf16[40,276,320,2]{1,0,3,2:T(8,128)(2,1)}), bf16[40,276,320,2]{1,0,3,2:T(8,128)(2,1)}, u32[]{:S(2)}, u32[]{:S(2)}) async-start(bf16[40,276,320,2]{1,0,3,2:T(8,128)(2,1)} %reshape.263), calls=%async_computation | async-start | bytes 39321600 | tf_op jit(solution)/shard_map/all_to_all | solution.py:70
  1416.9 15.0 copy-start.3
  1457.4 26.5 %copy-start.4 = (f32[69]{0:T(128)S(1)}, f32[69]{0:T(128)}, u32[]{:S(2)}) copy-start(f32[69]{0:T(128)} %param.15) | copy-start | bytes 832
  1866.0 17.2 copy-start.2
  1972.6 501.8 %all-to-all-start.1 = ((bf16[640,276,20,2]{1,3,2,0:T(2,128)(2,1)}), bf16[640,276,20,2]{1,3,2,0:T(2,128)(2,1)}, u32[]{:S(2)}, u32[]{:S(2)}) async-start(bf16[640,276,20,2]{1,3,2,0:T(2,128)(2,1)} %copy.42), calls=%async_computation.1 | async-start | bytes 39321600 | tf_op jit(solution)/shard_map/all_to_all | solution.py:73
  2493.3 107.6 %copy-start.1 = (s32[640]{0:T(1024)S(1)}, s32[640]{0:T(1024)}, u32[]{:S(2)}) copy-start(s32[640]{0:T(1024)} %param.10) | copy-start | bytes 7684
where the time goes:
time: 2620 us; the launch traced here: 2600 us
  other arithmetic  1270 us (48%)
  blocking collectives  446 us (17%)
  waiting for transfers between devices  381 us (15%)
  local copies, waits for them, and re-layouts  287 us (11%)
  matrix products  202 us (8%)
    another operation x1, other arithmetic  1190 us
    psum x1, blocking collectives, per_device(): loss_sum = lax.psum(partial_piece, ('lat', 'fld'))  446 us
    all_to_all x1, waiting for transfers between devices, send_out(): lax.all_to_all(values, 'lat', split_axis=2, concat_axis=0, tiled=True)  381 us
    dot_general x1, matrix products, per_device(): jnp.einsum('bcrk,rkj->rbcj', grid[0], tables, preferred_element_type=jnp....  88 us
    dot_general x1, matrix products, per_device(): jnp.einsum('rbj,rkj->brk', returned, tables, preferred_element_type=jnp.f...  72 us
  transfers between devices with their start and end apart: 2, of which 1 were waited for; matrix products, arithmetic and copies ran while one was open for 4% of the time, Pallas kernels for 0%

commit v1 on v0

v1 whole, which is shorter than its diff:
```python
import functools
import math

import jax
import jax.numpy as jnp
from jax import lax
from jax.experimental import pallas as pl
from jax.experimental.pallas import tpu as pltpu
from jax.sharding import PartitionSpec as P

STEPS = 2
KB = 256
GROUP = 8
LANES = 128


def round_up(value, unit):
    return (value + unit - 1) // unit * unit


def phasor_rows(lengths, wave_ids, block_count, wave_pad):
    exponents = [1 << bit for bit in range(8)] + [KB * block for block in range(block_count)]
    exponents = jnp.asarray(exponents, dtype=jnp.int32)
    length = lengths[:, None, None]
    phase = (exponents[None, :, None] * wave_ids[None, None, :]) % length
    length_f = length.astype(jnp.float32)
    turn = phase.astype(jnp.float32) / length_f
    quarter = jnp.floor(turn * 4.0 + 0.5)
    x = (turn - 0.25 * quarter) * jnp.float32(2.0 * math.pi)
    x2 = x * x
    sin_x = x * (1.0 + x2 * (-1.0 / 6 + x2 * (1.0 / 120 + x2 * (-1.0 / 5040 + x2 * (1.0 / 362880)))))
    cos_x = 1.0 + x2 * (
        -0.5 + x2 * (1.0 / 24 + x2 * (-1.0 / 720 + x2 * (1.0 / 40320 + x2 * (-1.0 / 3628800))))
    )
    odd = (quarter == 1.0) | (quarter == 3.0)
    cos_t = jnp.where(odd, sin_x, cos_x)
    cos_t = jnp.where((quarter == 1.0) | (quarter == 2.0), -cos_t, cos_t)
    sin_t = jnp.where(odd, cos_x, sin_x)
    sin_t = jnp.where((quarter == 2.0) | (quarter == 3.0), -sin_t, sin_t)
    scale = jnp.where(2 * wave_ids[None, None, :] < length, lax.rsqrt(length_f), jnp.float32(0.0))
    lane_pad = ((0, 0), (0, 0), (0, wave_pad - wave_ids.shape[0]))
    cos_t = jnp.concatenate([cos_t, scale], axis=1)
    sin_t = jnp.concatenate([-sin_t, jnp.zeros_like(scale)], axis=1)
    rows = jnp.concatenate([jnp.pad(cos_t, lane_pad), jnp.pad(sin_t, lane_pad)], axis=2)
    row_pad = round_up(rows.shape[1], 8) - rows.shape[1]
    return jnp.pad(rows, ((0, 0), (0, row_pad), (0, 0)))


def rotate(cos_a, sin_a, cos_b, sin_b):
    return cos_a * cos_b - sin_a * sin_b, cos_a * sin_b + sin_a * cos_b


def build_base(ph_ref, base_ref, slot, wave_pad, scale_row):
    row = lax.broadcasted_iota(jnp.int32, (8, wave_pad), 0)
    cos_v = jnp.broadcast_to(ph_ref[slot, scale_row : scale_row + 1, :wave_pad], (8, wave_pad))
    sin_v = jnp.zeros((8, wave_pad), jnp.float32)
    for bit in range(3):
        on = ((row >> bit) & 1) == 1
        cos_b = jnp.where(on, ph_ref[slot, bit : bit + 1, :wave_pad], 1.0)
        sin_b = jnp.where(on, ph_ref[slot, bit : bit + 1, wave_pad:], 0.0)
        cos_v, sin_v = rotate(cos_v, sin_v, cos_b, sin_b)
    base_ref[0:8, :wave_pad] = cos_v
    base_ref[0:8, wave_pad:] = sin_v
    size, bit = 8, 3
    while size < KB:
        cos_b = ph_ref[slot, bit : bit + 1, :wave_pad]
        sin_b = ph_ref[slot, bit : bit + 1, wave_pad:]
        for start in range(0, size, 32):
            stop = min(start + 32, size)
            cos_v, sin_v = rotate(
                base_ref[start:stop, :wave_pad], base_ref[start:stop, wave_pad:], cos_b, sin_b
            )
            base_ref[size + start : size + stop, :wave_pad] = cos_v
            base_ref[size + start : size + stop, wave_pad:] = sin_v
        size, bit = size * 2, bit + 1


def table_block(ph_ref, base_ref, table_ref, slot, block, wave_pad):
    turn = ph_ref[slot, pl.ds(8 + block, 1), :]
    cos_b, sin_b = turn[:, :wave_pad], turn[:, wave_pad:]
    for start in range(0, KB, 32):
        stop = start + 32
        cos_v, sin_v = rotate(
            base_ref[start:stop, :wave_pad], base_ref[start:stop, wave_pad:], cos_b, sin_b
        )
        table_ref[start:stop, :wave_pad] = cos_v.astype(jnp.bfloat16)
        table_ref[start:stop, wave_pad:] = sin_v.astype(jnp.bfloat16)


def forward_kernel(
    wave_count, wave_pad, scale_row, groups, rest, len_ref, ph_ref, *refs
):
    if rest:
        grid_ref, grid_rest_ref, out_ref, base_ref, table_ref, wide_ref, acc_ref, rows_ref, wide_rest_ref, rest_ref = refs
        rest_cols = grid_rest_ref.shape[0]
        per_row = LANES // rest
        rest_rows = rest_ref.shape[0] // (2 * wave_count)
    else:
        grid_ref, out_ref, base_ref, table_ref, wide_ref, acc_ref, rows_ref = refs
        rest_cols = 0
    group = pl.program_id(0)
    segment = grid_ref.shape[2]
    owners, _, wave_dev = out_ref.shape[:3]

    def store_rows(source):
        for part in range(2):
            rows = source[part * wave_count * GROUP : (part + 1) * wave_count * GROUP, :]
            out_ref[:, part] = rows.reshape(owners, wave_dev, GROUP, LANES).astype(jnp.bfloat16)

    def run_group():
        for lane in range(segment // LANES):
            piece = grid_ref[:, :, lane * LANES : (lane + 1) * LANES].astype(jnp.float32)
            wide_ref[lane] = piece.reshape(LANES * GROUP, LANES)
            if rest:
                piece = grid_rest_ref[:, :, lane * LANES : (lane + 1) * LANES].astype(jnp.float32)
                wide_rest_ref[lane] = piece.reshape(rest_cols * GROUP, LANES)

        def per_slot(slot, carry):
            length = len_ref[group * GROUP + slot]
            build_base(ph_ref, base_ref, slot, wave_pad, scale_row)
            acc_ref[...] = jnp.zeros_like(acc_ref)

            def per_block(block, inner):
                table_block(ph_ref, base_ref, table_ref, slot, block, wave_pad)
                pieces = []
                for part in range(KB // LANES):
                    lane_block = block * (KB // LANES) + part
                    values = wide_ref[lane_block, pl.ds(slot, LANES, stride=GROUP), :]
                    if rest:
                        extra = wide_rest_ref[lane_block, pl.ds(slot, rest_cols, stride=GROUP), :]
                        values = jnp.concatenate([values, extra], axis=0)
                    at = lane_block * LANES + lax.broadcasted_iota(jnp.int32, values.shape, 1)
                    pieces.append(jnp.where(at < length, values, 0.0).astype(jnp.bfloat16))
                acc_ref[...] += jnp.dot(
                    jnp.concatenate(pieces, axis=1), table_ref[...], preferred_element_type=jnp.float32
                )
                return inner

            lax.fori_loop(0, (length + KB - 1) // KB, per_block, 0)
            for part in range(2):
                lanes = slice(part * wave_pad, (part + 1) * wave_pad)
                turned = acc_ref[:LANES, lanes].T
                rows_ref[pl.ds(part * wave_count * GROUP + slot, wave_count, stride=GROUP), :] = (
                    turned[:wave_count]
                )
                if rest:
                    cycle = group * GROUP + slot
                    turned = acc_ref[LANES:, lanes].T[:wave_count]
                    fill = jnp.zeros((wave_count, LANES - rest_cols), jnp.float32)
                    turned = jnp.concatenate([turned, fill], axis=1)
                    keep = lax.broadcasted_iota(jnp.int32, turned.shape, 1) < rest
                    turned = jnp.where(keep, turned, 0.0)
                    turned = pltpu.roll(turned, lax.rem(cycle, per_row) * rest, 1)
                    at = pl.ds(part * wave_count * rest_rows + cycle // per_row, wave_count, stride=rest_rows)
                    rest_ref[at, :] += turned
            return carry

        lax.fori_loop(0, GROUP, per_slot, 0)
        store_rows(rows_ref)

    if rest:

        @pl.when(group == 0)
        def _():
            rest_ref[...] = jnp.zeros_like(rest_ref)

        pl.when(group < groups)(run_group)

        @pl.when(group == groups)
        def _():
            store_rows(rest_ref)
    else:
        run_group()


def forward_dft(grid, lengths, phasors, owners, wave_count, wave_pad, scale_row, chunk):
    index, rest, rest_cols, rest_index = chunk
    col_count, cycle_dev, segment = grid.shape
    groups = pl.cdiv(cycle_dev, GROUP)
    wide_lanes = round_up(segment, KB) // LANES
    wave_dev = wave_count // owners
    rows = (groups + (1 if rest else 0)) * GROUP
    last = groups - 1
    in_specs = [
        pl.BlockSpec((GROUP,) + phasors.shape[1:], lambda g, n: (jnp.minimum(g, last), 0, 0)),
        pl.BlockSpec((LANES, GROUP, segment), lambda g, n: (index, jnp.minimum(g, last), 0)),
    ]
    operands = [lengths, phasors, grid]
    scratch = [
        pltpu.VMEM((KB, 2 * wave_pad), jnp.float32),
        pltpu.VMEM((KB, 2 * wave_pad), jnp.bfloat16),
        pltpu.VMEM((wide_lanes, LANES * GROUP, LANES), jnp.float32),
        pltpu.VMEM((LANES + rest_cols, 2 * wave_pad), jnp.float32),
        pltpu.VMEM((2 * wave_count * GROUP, LANES), jnp.float32),
    ]
    if rest:
        in_specs.append(
            pl.BlockSpec((rest_cols, GROUP, segment), lambda g, n: (rest_index, jnp.minimum(g, last), 0))
        )
        operands.append(grid)
        scratch += [
            pltpu.VMEM((wide_lanes, rest_cols * GROUP, LANES), jnp.float32),
            pltpu.VMEM((2 * wave_count * GROUP, LANES), jnp.float32),
        ]
    return pl.pallas_call(
        functools.partial(forward_kernel, wave_count, wave_pad, scale_row, groups, rest),
        out_shape=jax.ShapeDtypeStruct((owners, 2, wave_dev, rows, LANES), jnp.bfloat16),
        grid_spec=pltpu.PrefetchScalarGridSpec(
            num_scalar_prefetch=1,
            grid=(rows // GROUP,),
            in_specs=in_specs,
            out_specs=pl.BlockSpec((owners, 2, wave_dev, GROUP, LANES), lambda g, n: (0, 0, 0, g, 0)),
            scratch_shapes=scratch,
        ),
        compiler_params=pltpu.CompilerParams(
            dimension_semantics=("arbitrary",), vmem_limit_bytes=56 * 1024 * 1024
        ),
        cost_estimate=pl.CostEstimate(
            flops=2 * LANES * cycle_dev * segment * wave_pad,
            bytes_accessed=2 * LANES * cycle_dev * (segment + 2 * wave_count),
            transcendentals=0,
        ),
        name="forward_dft",
    )(*operands)


def adjoint_kernel(wave_count, wave_pad, scale_row, rest, aliased, len_ref, ph_ref, *refs):
    refs = list(refs)
    back_ref = refs.pop(0)
    back_rest_ref = refs.pop(0) if rest else None
    if aliased:
        refs.pop(0)
    out_ref = refs.pop(0)
    out_rest_ref = refs.pop(0) if rest else None
    base_ref, table_ref, lhs_ref, rows_ref, wide_ref = refs[:5]
    if rest:
        wide_rest_ref, rest_ref = refs[5:]
        rest_cols = out_rest_ref.shape[0]
        per_row = LANES // rest
    group = pl.program_id(0)
    segment = out_ref.shape[2]
    lane_count = wide_ref.shape[0]
    per_kb = KB // LANES
    span = wave_count * GROUP
    for part in range(2):
        rows_ref[part * span : (part + 1) * span, :] = (
            back_ref[:, part].astype(jnp.float32).reshape(span, LANES)
        )

    @pl.when(group == 0)
    def _():
        lhs_ref[...] = jnp.zeros_like(lhs_ref)
        if rest:
            for part in range(2):
                rest_ref[part * span : (part + 1) * span, :] = (
                    back_rest_ref[:, part].astype(jnp.float32).reshape(span, LANES)
                )

    def put(slot, lane_block, values):
        wide_ref[lane_block, pl.ds(slot, LANES, stride=GROUP), :] = values[:LANES]
        if rest:
            wide_rest_ref[lane_block, pl.ds(slot, rest_cols, stride=GROUP), :] = values[LANES:]

    def per_slot(slot, carry):
        length = len_ref[group * GROUP + slot]
        build_base(ph_ref, base_ref, slot, wave_pad, scale_row)
        for part in range(2):
            lanes = slice(part * wave_pad, part * wave_pad + wave_count)
            turned = rows_ref[pl.ds(part * span + slot, wave_count, stride=GROUP), :].T
            lhs_ref[:LANES, lanes] = turned.astype(jnp.bfloat16)
            if rest:
                cycle = group * GROUP + slot
                rows = rest_ref[pl.ds(part * span + cycle // per_row, wave_count, stride=GROUP), :]
                rows = pltpu.roll(rows, LANES - lax.rem(cycle, per_row) * rest, 1)
                lhs_ref[LANES:, lanes] = rows[:, :rest_cols].T.astype(jnp.bfloat16)
        used = (length + KB - 1) // KB

        def per_block(block, inner):
            table_block(ph_ref, base_ref, table_ref, slot, block, wave_pad)
            values = lax.dot_general(
                lhs_ref[...], table_ref[...], (((1,), (1,)), ((), ())), preferred_element_type=jnp.float32
            )
            for part in range(per_kb):
                lane_block = block * per_kb + part
                piece = values[:, part * LANES : (part + 1) * LANES]
                at = lane_block * LANES + lax.broadcasted_iota(jnp.int32, piece.shape, 1)
                put(slot, lane_block, jnp.where(at < length, piece, 0.0))
            return inner

        def fill(lane_block, inner):
            put(slot, lane_block, jnp.zeros((lhs_ref.shape[0], LANES), jnp.float32))
            return inner

        lax.fori_loop(0, used, per_block, 0)
        lax.fori_loop(used * per_kb, lane_count, fill, 0)
        return carry

    lax.fori_loop(0, GROUP, per_slot, 0)
    for lane in range(segment // LANES):
        lanes = slice(lane * LANES, (lane + 1) * LANES)
        out_ref[:, :, lanes] = wide_ref[lane].reshape(LANES, GROUP, LANES).astype(jnp.bfloat16)
        if rest:
            values = wide_rest_ref[lane].reshape(rest_cols, GROUP, LANES)
            out_rest_ref[:, :, lanes] = values.astype(jnp.bfloat16)


def adjoint_dft(back, field, lengths, phasors, out_shape, wave_count, wave_pad, scale_row, chunk):
    index, rest, rest_cols, rest_index = chunk
    col_count, cycle_dev, segment = out_shape
    owners, _, wave_dev, rows, _ = back.shape
    groups = pl.cdiv(cycle_dev, GROUP)
    wide_lanes = round_up(segment, KB) // LANES
    aliased = field is not None
    block = (owners, 2, wave_dev, GROUP, LANES)
    in_specs = [
        pl.BlockSpec((GROUP,) + phasors.shape[1:], lambda g, n: (g, 0, 0)),
        pl.BlockSpec(block, lambda g, n: (0, 0, 0, g, 0)),
    ]
    operands = [lengths, phasors, back]
    out_specs = [pl.BlockSpec((LANES, GROUP, segment), lambda g, n: (index, g, 0))]
    out_shapes = [jax.ShapeDtypeStruct(out_shape, jnp.bfloat16)]
    scratch = [
        pltpu.VMEM((KB, 2 * wave_pad), jnp.float32),
        pltpu.VMEM((KB, 2 * wave_pad), jnp.bfloat16),
        pltpu.VMEM((LANES + rest_cols, 2 * wave_pad), jnp.bfloat16),
        pltpu.VMEM((2 * wave_count * GROUP, LANES), jnp.float32),
        pltpu.VMEM((wide_lanes, LANES * GROUP, LANES), jnp.float32),
    ]
    if rest:
        in_specs.append(pl.BlockSpec(block, lambda g, n: (0, 0, 0, groups, 0)))
        operands.append(back)
        out_specs.append(pl.BlockSpec((rest_cols, GROUP, segment), lambda g, n: (0, g, 0)))
        out_shapes.append(jax.ShapeDtypeStruct((rest_cols, cycle_dev, segment), jnp.bfloat16))
        scratch += [
            pltpu.VMEM((wide_lanes, rest_cols * GROUP, LANES), jnp.float32),
            pltpu.VMEM((2 * wave_count * GROUP, LANES), jnp.float32),
        ]
    aliases = {}
    if aliased:
        aliases = {len(operands): 0}
        in_specs.append(pl.BlockSpec(memory_space=pl.ANY))
        operands.append(field)
    return pl.pallas_call(
        functools.partial(adjoint_kernel, wave_count, wave_pad, scale_row, rest, aliased),
        out_shape=out_shapes,
        grid_spec=pltpu.PrefetchScalarGridSpec(
            num_scalar_prefetch=1, grid=(groups,), in_specs=in_specs, out_specs=out_specs, scratch_shapes=scratch
        ),
        input_output_aliases=aliases,
        compiler_params=pltpu.CompilerParams(
            dimension_semantics=("arbitrary",), vmem_limit_bytes=60 * 1024 * 1024
        ),
        cost_estimate=pl.CostEstimate(
            flops=2 * LANES * cycle_dev * segment * wave_pad,
            bytes_accessed=2 * LANES * cycle_dev * (segment + 2 * wave_count),
            transcendentals=0,
        ),
        name="adjoint_dft",
    )(*operands)


def column_chunks(col_count):
    whole = col_count // LANES
    rest = col_count - whole * LANES
    chunks = [(index, 0, 0, 0) for index in range(whole)]
    if rest:
        width = 8
        while width < rest:
            width *= 2
        chunks[-1] = (whole - 1, rest, width, whole * LANES // width)
    return chunks


def per_device(grid, cycle_ids, cycle_len, wave_ids, legendre, target, step_w, chan_w):
    _, batch_size, chan_count, cycle_dev, segment = grid.shape
    wave_count = wave_ids.shape[0]
    wave_dev, degree_count, cycle_count = legendre.shape
    owners = wave_count // wave_dev
    col_count = batch_size * chan_count
    wave_pad = round_up(wave_count, LANES)
    block_count = pl.cdiv(segment, KB)
    scale_row = 8 + block_count
    lat_index = lax.axis_index("lat")
    my_cycles = lax.dynamic_slice_in_dim(cycle_ids, lat_index * cycle_dev, cycle_dev)
    lengths = jnp.take(cycle_len, my_cycles)
    phasors = phasor_rows(lengths, wave_ids, block_count, wave_pad)
    group_pad = round_up(cycle_dev, GROUP) - cycle_dev
    if group_pad:
        lengths = jnp.pad(lengths, (0, group_pad))
        phasors = jnp.pad(phasors, ((0, group_pad), (0, 0), (0, 0)))
    grid3 = grid.reshape(col_count, cycle_dev, segment)
    my_waves = lax.dynamic_slice_in_dim(wave_ids, lat_index * wave_dev, wave_dev)
    degree = jnp.arange(degree_count, dtype=jnp.int32)
    kept = (degree[None, :] >= my_waves[:, None]).astype(jnp.float32)[:, :, None, None]
    factor = jnp.where(my_waves == 0, 1.0, 2.0).astype(jnp.float32)
    weight_cols = jnp.broadcast_to(step_w[0] * chan_w[None, :], (batch_size, chan_count)).reshape(
        col_count
    )
    target3 = target.reshape(col_count, 2, wave_dev, degree_count)

    def exchange(values):
        shape = values.shape
        flat = values.reshape((owners * 2 * wave_dev,) + shape[3:])
        return lax.all_to_all(flat, "lat", split_axis=0, concat_axis=0, tiled=True).reshape(shape)

    chunks = column_chunks(col_count)
    groups = pl.cdiv(cycle_dev, GROUP)
    sent = []
    for chunk in chunks:
        part = forward_dft(grid3, lengths, phasors, owners, wave_count, wave_pad, scale_row, chunk)
        part, lengths, legendre, target3 = lax.optimization_barrier((part, lengths, legendre, target3))
        sent.append(part)
    legendre_cols = jnp.take(legendre, cycle_ids, axis=2).reshape(
        wave_dev, degree_count, owners, cycle_dev
    )

    def owner_pass(gathered, start, cols):
        coeffs = jnp.einsum(
            "sndp,dtspc->sntc", legendre_cols, gathered, preferred_element_type=jnp.float32
        )
        coeffs = coeffs * kept
        goal = jnp.transpose(target3[start : start + cols], (2, 3, 1, 0))
        weight = factor[:, None, None, None] * weight_cols[None, None, None, start : start + cols]
        misfit = (coeffs - goal) * kept
        value = jnp.sum(weight * misfit * misfit)
        grad_coeff = (2.0 * weight * misfit).astype(jnp.bfloat16)
        back = jnp.einsum(
            "sndp,sntc->dtspc", legendre_cols, grad_coeff, preferred_element_type=jnp.float32
        ).astype(jnp.bfloat16)
        return jnp.transpose(coeffs, (3, 2, 0, 1)), value, back

    partial_value = jnp.float32(0.0)
    coeff_parts, backs = [], []
    for chunk, part in zip(chunks, sent):
        index, rest = chunk[:2]
        gathered = exchange(part)
        coeff_part, value, back = owner_pass(gathered[:, :, :, :cycle_dev], index * LANES, LANES)
        coeff_parts.append(coeff_part)
        partial_value = partial_value + value
        row_pad = groups * GROUP - cycle_dev
        if row_pad:
            back = jnp.pad(back, ((0, 0),) * 3 + ((0, row_pad), (0, 0)))
        if rest:
            per_row = LANES // rest
            lead = gathered.shape[:3]
            packed = gathered[:, :, :, groups * GROUP :, : per_row * rest]
            unpacked = packed.reshape(lead + (GROUP * per_row, rest))[:, :, :, :cycle_dev]
            coeff_part, value, back_rest = owner_pass(unpacked, col_count - rest, rest)
            coeff_parts.append(coeff_part)
            partial_value = partial_value + value
            back_rest = jnp.pad(back_rest, ((0, 0),) * 3 + ((0, GROUP * per_row - cycle_dev), (0, 0)))
            back_rest = back_rest.reshape(lead + (GROUP, per_row * rest))
            back_rest = jnp.pad(back_rest, ((0, 0),) * 4 + ((0, LANES - per_row * rest),))
            back = jnp.concatenate([back, back_rest], axis=3)
        backs.append(back)
    loss_sum = lax.psum(partial_value, ("lat", "fld"))
    backs[-1], loss_sum = lax.optimization_barrier((backs[-1], loss_sum))
    field = None
    for chunk, back in zip(chunks, backs):
        returned = exchange(back)
        results = adjoint_dft(
            returned, field, lengths, phasors, grid3.shape, wave_count, wave_pad, scale_row, chunk
        )
        field = results[0]
        if chunk[1]:
            field = lax.dynamic_update_slice(field, results[1][: chunk[1]], (col_count - chunk[1], 0, 0))
    coeff_out = jnp.concatenate(coeff_parts, axis=0)
    term_count = STEPS * col_count * wave_count * (wave_count + 1) // 2
    loss = loss_sum / jnp.float32(term_count)
    return (
        coeff_out.reshape(1, batch_size, chan_count, 2, wave_dev, degree_count),
        loss,
        field.reshape(1, batch_size, chan_count, cycle_dev, segment),
    )


def solution(mesh):
    return jax.shard_map(
        per_device,
        mesh=mesh,
        in_specs=(
            P("fld", None, None, "lat", None),
            P(),
            P(),
            P(),
            P("lat", None, None),
            P("fld", None, None, None, "lat", None),
            P("fld"),
            P(),
        ),
        out_specs=(P("fld", None, None, None, "lat", None), P(), P("fld", None, None, "lat", None)),
        check_vma=False,
    )
```

time: 2620 us -> 915 us (0.35)
  other arithmetic: 1270 us -> 58.8 us
  blocking collectives: 446 us -> 103 us
  Pallas kernels: 0 us -> 277 us
  waiting for transfers between devices: 381 us -> 203 us
  local copies, waits for them, and re-layouts: 287 us -> 154 us
  matrix products: 202 us -> 75.1 us
    another operation x2 -> x0, other arithmetic: 1240 us -> none
    psum x1, blocking collectives: 446 us -> 103 us  [per_device(): loss_sum = lax.psum(partial_value, ('lat', 'fld'))]
    pallas_call x0 -> x4, Pallas kernels: none -> 277 us  [the longest x2 145 us: adjoint_dft(): pl.pallas_call(functools.partial(adjoint_kernel, wave_count, wave_pad, sc...]
    all_to_all x2 -> x4, waiting for transfers between devices: 381 us -> 203 us  [exchange(): lax.all_to_all(flat, 'lat', split_axis=0, concat_axis=0, tiled=True)]
    dot_general x4 -> x6, matrix products: 202 us -> 75.1 us  [the longest x3 39.3 us: owner_pass(): jnp.einsum('sndp,sntc->dtspc', legendre_cols, grad_coeff, preferred_eleme...]
    convert_element_type x3 -> x1, local copies, waits for them, and re-layouts: 124 us -> 7.28 us  [owner_pass(): back = jnp.einsum('sndp,sntc->dtspc', legendre_cols, grad_coeff, preferre...]
    optimization_barrier x0 -> x3, local copies, waits for them, and re-layouts: none -> 46.8 us  [the longest x2 41.4 us: per_device(): lax.optimization_barrier((part, lengths, legendre, target3))]
    all_to_all x3 -> x0, local copies, waits for them, and re-layouts: 36.1 us -> none  [the longest x2 18.9 us: send_back(): lax.all_to_all(values, 'lat', split_axis=0, concat_axis=2, tiled=True)]
  transfers between devices with their start and end apart: 2 -> 4, of which waited for: 1 -> 3; matrix products, arithmetic and copies ran while one was open for 4% -> 30% of each run, Pallas kernels for 0% -> 16%
where the time goes in v1:
time: 915 us; the launch traced here: 904 us
  Pallas kernels  277 us (30%)
  waiting for transfers between devices  203 us (22%)
  local copies, waits for them, and re-layouts  154 us (17%)
  blocking collectives  103 us (11%)
  matrix products  75.1 us (8%)
  other arithmetic  58.8 us (6%)
  starting transfers between devices  26.3 us (3%)
    all_to_all x4, waiting for transfers between devices, exchange(): lax.all_to_all(flat, 'lat', split_axis=0, concat_axis=0, tiled=True)  203 us
    pallas_call x2, Pallas kernels, adjoint_dft(): pl.pallas_call(functools.partial(adjoint_kernel, wave_count, wave_pad, sc...  145 us
    pallas_call x2, Pallas kernels, forward_dft(): pl.pallas_call(functools.partial(forward_kernel, wave_count, wave_pad, sc...  132 us
    psum x1, blocking collectives, per_device(): loss_sum = lax.psum(partial_value, ('lat', 'fld'))  103 us
    optimization_barrier x2, local copies, waits for them, and re-layouts, per_device(): lax.optimization_barrier((part, lengths, legendre, target3))  41.4 us
    dot_general x3, matrix products, owner_pass(): jnp.einsum('sndp,sntc->dtspc', legendre_cols, grad_coeff, preferred_eleme...  39.3 us
    dot_general x3, matrix products, owner_pass(): jnp.einsum('sndp,dtspc->sntc', legendre_cols, gathered, preferred_element...  35.8 us
    gather x2, local copies, waits for them, and re-layouts, per_device(): jnp.take(legendre, cycle_ids, axis=2)  35.4 us
  transfers between devices with their start and end apart: 4, of which 3 were waited for; matrix products, arithmetic and copies ran while one was open for 30% of the time, Pallas kernels for 16%

profile of v1, /device:TPU:28, one launch (start us, length us, event | category | flops | bytes accessed | tf_op | source)
XLA Modules:
  0.0 904.1 jit_solution(8159010352912931111)
XLA Ops:
  4.6 10.9 %negate_select_fusion.1 = (f32[40,14,320]{2,1,0:T(8,128)S(1)}, f32[40,14,320]{2,1,0:T(8,128)S(1)}) fusion(f32[40]{0:T(128)S(1)} %get-tuple-element.53, pred[40]{0:T(512)(128)(4,1)S(1)} %broadcast_compare_fusion, s32[40]{0:T(128)S(1)} %get-tuple-element.52, s32[14,320]{1,0:T(8,128)S(1)} %broadcast_multiply_fusion), kind=kLoop, calls=%fused_computation.65 | loop fusion | flops 8601600 | bytes 1451880 | tf_op jit(solution)/shard_map/jit(_where)/select_n | solution.py:37
  17.6 60.0 %forward_dft.2 = bf16[16,2,20,40,128]{4,3,2,1,0:T(8,128)(2,1)} custom-call(s32[40]{0:T(128)} %copy-done.3, f32[40,16,768]{2,1,0:T(8,128)} %pad.22.ph_ref, bf16[276,40,1408]{2,1,0:T(8,128)(2,1)} %bitcast.144), custom_call_target="tpu_custom_call" | custom-call | flops 5536481280 | bytes 20971520 | tf_op jit(solution)/shard_map/forward_dft/pallas_call | solution.py:205
  77.5 6.0 all-to-all-start
  83.6 72.4 %forward_dft.3 = bf16[16,2,20,48,128]{4,3,2,1,0:T(8,128)(2,1)} custom-call(s32[40]{0:T(128)} %copy-done.3, f32[40,16,768]{2,1,0:T(8,128)} %pad.22.ph_ref, bf16[276,40,1408]{2,1,0:T(8,128)(2,1)} %bitcast.145, bf16[276,40,1408]{2,1,0:T(8,128)(2,1)} %bitcast.146), custom_call_target="tpu_custom_call" | custom-call | flops 5536481280 | bytes 20971520 | tf_op jit(solution)/shard_map/forward_dft/pallas_call | solution.py:205
  156.0 76.0 %all-to-all-done = bf16[640,40,128]{2,1,0:T(8,128)(2,1)} async-done(((bf16[640,40,128]{2,1,0:T(8,128)(2,1)}), bf16[640,40,128]{2,1,0:T(8,128)(2,1)}, u32[]{:S(2)}, u32[]{:S(2)}) %all-to-all-start) | async-done | bytes 6553632 | tf_op jit(solution)/shard_map/all_to_all | solution.py:404
  232.0 6.1 all-to-all-start.1
  239.0 15.0 %copy.20 = bf16[20,320,640]{1,0,2:T(8,128)(2,1)} copy(bf16[20,320,640]{2,1,0:T(8,128)(2,1)} %param.13) | data formatting | bytes 16384000 | tf_op jit(solution)/shard_map/optimization_barrier | solution.py:411
  254.0 25.5 %gather_fusion.1 = bf16[640,20,320]{2,1,0:T(8,128)(2,1)} fusion(bf16[20,320,640]{1,0,2:T(8,128)(2,1)} %copy.20, s32[1024]{0:T(1024)S(1)} %pad_clamp_fusion), kind=kCustom, calls=%fused_computation.1 | custom fusion | bytes 16386560 | tf_op jit(solution)/shard_map/jit(_take)/gather | solution.py:413
  279.5 9.9 %copy.21 = bf16[20,320,640]{1,2,0:T(8,128)(2,1)} copy(bf16[20,320,640]{1,0,2:T(8,128)(2,1)} %bitcast.148) | data formatting | bytes 16384000 | tf_op jit(solution)/shard_map/jit(_take)/gather | solution.py:413
  289.4 26.5 %copy.27 = f32[276,2,20,320]{0,3,1,2:T(8,128)} copy(f32[276,2,20,320]{3,1,2,0:T(2,128)} %bitcast.153) | data formatting | bytes 28262400 | tf_op jit(solution)/shard_map/optimization_barrier | solution.py:411
  316.8 12.0 %fusion.11 = f32[20,320,2,128,1]{3,1,4,2,0:T(8,128)} fusion(bf16[16,2,20,40,128]{4,3,2,1,0:T(8,128)(2,1)} %bitcast.7, bf16[20,320,16,40]{1,3,2,0:T(8,128)(2,1)} %bitcast.155, pred[16,40]{1,0:T(8,128)(4,1)S(1)} %broadcast_in_dim.66), kind=kOutput, calls=%fused_computation.15 | convolution fusion | flops 2101248000 | bytes 21299840 | tf_op jit(solution)/shard_map/sndp,dtspc->sntc/dot_general | solution.py:418
  328.8 12.0 %fusion.35 = bf16[16,2,20,40,128]{4,3,0,1,2:T(8,128)(2,1)} fusion(bf16[20,320,16,40]{1,3,2,0:T(8,128)(2,1)} %bitcast.156, pred[16,40]{1,0:T(8,128)(4,1)S(1)} %broadcast_in_dim.66, f32[20,128]{1,0:T(8,128)S(1)} %get-tuple-element.44, f32[276,2,20,320]{0,3,1,2:T(8,128)} %copy.27, f32[20,320,2,128,1]{3,1,4,2,0:T(8,128)} %fusion.11, f32[20,320]{1,0:T(8,128)S(1)} %fusion.67), kind=kOutput, calls=%fused_computation.48 | convolution fusion | flops 2112716800 | bytes 29527680 | tf_op jit(solution)/shard_map/sndp,sntc->dtspc/dot_general | solution.py:427
  340.7 7.3 copy.34
  348.0 64.9 %all-to-all-done.1 = bf16[640,48,128]{2,1,0:T(8,128)(2,1)} async-done(((bf16[640,48,128]{2,1,0:T(8,128)(2,1)}), bf16[640,48,128]{2,1,0:T(8,128)(2,1)}, u32[]{:S(2)}, u32[]{:S(2)}) %all-to-all-start.1) | async-done | bytes 7864352 | tf_op jit(solution)/shard_map/all_to_all | solution.py:404
  412.9 6.3 all-to-all-start.3
  420.8 7.0 reshape.371
  427.8 11.9 %fusion.9 = f32[20,320,2,128,1]{3,1,4,2,0:T(8,128)} fusion(bf16[20,320,16,40]{1,3,2,0:T(8,128)(2,1)} %bitcast.157, pred[16,40]{1,0:T(8,128)(4,1)S(1)} %broadcast_in_dim.66, bf16[16,2,20,48,128]{4,3,2,1,0:T(8,128)(2,1)} %bitcast.13), kind=kOutput, calls=%fused_computation.13 | convolution fusion | flops 2101248000 | bytes 22938240 | tf_op jit(solution)/shard_map/sndp,dtspc->sntc/dot_general | solution.py:418
  439.7 15.4 %fusion.21 = (f32[]{:T(128)}, f32[]{:T(128)}, f32[128,2,20,320]{0,3,1,2:T(8,128)}, f32[128,2,20,320]{0,3,1,2:T(8,128)}) fusion(f32[20,128]{1,0:T(8,128)S(1)} %get-tuple-element.51, f32[276,2,20,320]{0,3,1,2:T(8,128)} %copy.27, f32[20,320]{1,0:T(8,128)S(1)} %fusion.67, f32[20,320,2,128,1]{3,1,4,2,0:T(8,128)} %fusion.9, f32[20,320,2,128,1]{3,1,4,2,0:T(8,128)} %fusion.11, ...), kind=kLoop, calls=%fused_computation.25 | loop fusion | flops 19660800 | bytes 39367688 | tf_op jit(solution)/shard_map/reduce_sum | solution.py:425
  456.5 11.9 %fusion.7 = f32[20,320,2,20,1]{3,1,4,2,0:T(8,128)} fusion(bf16[20,320,16,40]{1,3,2,0:T(8,128)(2,1)} %bitcast.158, pred[16,40]{1,0:T(8,128)(4,1)S(1)} %broadcast_in_dim.66, bf16[16,2,20,48,20]{4,3,2,1,0:T(8,128)(2,1)} %reshape.371), kind=kOutput, calls=%fused_computation.11 | convolution fusion | flops 331776000 | bytes 17408640 | tf_op jit(solution)/shard_map/sndp,dtspc->sntc/dot_general | solution.py:418
  468.4 8.3 fusion.22
  477.4 103.4 %psum.7 = f32[]{:T(128)} all-reduce(f32[]{:T(128)S(6)} %add.132), channel_id=1, replica_groups=mesh['lat'=16,'fld'=2] {'lat','fld'}, use_global_device_ids=true, to_apply=%region_3.4 | all-reduce | flops 1 | bytes 8 | tf_op jit(solution)/shard_map/psum | solution.py:456
  580.8 15.4 %convert_bitcast_fusion = bf16[16,2,20,40,20]{3,4,0,1,2:T(8,128)(2,1)} fusion(bf16[20,320,16,40]{1,3,2,0:T(8,128)(2,1)} %bitcast.159, pred[16,40]{1,0:T(8,128)(4,1)S(1)} %broadcast_in_dim.66, f32[20,20]{1,0:T(8,128)S(1)} %get-tuple-element.47, f32[276,2,20,320]{0,3,1,2:T(8,128)} %copy.27, f32[20,320,2,20,1]{3,1,4,2,0:T(8,128)} %fusion.7, ...), kind=kOutput, calls=%fused_computation.50 | convolution fusion | flops 333568000 | bytes 23989440 | tf_op jit(solution)/shard_map/sndp,sntc->dtspc/dot_general | solution.py:427
  596.1 8.7 copy.49
  604.8 7.9 pad.23.clone
  612.7 8.8 reshape.405
  621.4 12.0 %fusion.38 = bf16[16,2,20,40,128]{4,3,0,1,2:T(8,128)(2,1)} fusion(bf16[20,320,16,40]{1,3,2,0:T(8,128)(2,1)} %bitcast.160, pred[16,40]{1,0:T(8,128)(4,1)S(1)} %broadcast_in_dim.66, f32[20,128]{1,0:T(8,128)S(1)} %get-tuple-element.50, f32[276,2,20,320]{0,3,1,2:T(8,128)} %copy.27, f32[20,320,2,128,1]{3,1,4,2,0:T(8,128)} %fusion.9, f32[20,320]{1,0:T(8,128)S(1)} %fusion.67), kind=kOutput, calls=%fused_computation.49 | convolution fusion | flops 2112716800 | bytes 29527680 | tf_op jit(solution)/shard_map/sndp,sntc->dtspc/dot_general | solution.py:427
  643.1 7.8 all-to-all-start.2
  650.9 15.2 %pad_maximum_fusion = f32[276,2,20,320]{0,3,1,2:T(8,128)} fusion(f32[20,2,20,320]{0,3,1,2:T(8,128)} %get-tuple-element.37, f32[128,2,20,320]{0,3,1,2:T(8,128)} %get-tuple-element.38, f32[128,2,20,320]{0,3,1,2:T(8,128)} %get-tuple-element.39), kind=kLoop, calls=%fused_computation.2 | loop fusion | flops 7065600 | bytes 28262400 | tf_op jit(solution)/shard_map/concatenate | solution.py:467
  666.1 25.6 %copy.26 = f32[276,2,20,320]{3,1,2,0:T(2,128)} copy(f32[276,2,20,320]{0,3,1,2:T(8,128)} %pad_maximum_fusion) | data formatting | bytes 28262400 | tf_op jit(solution)/shard_map/concatenate | solution.py:467
  692.3 68.0 %adjoint_dft.2.refs_2_ = bf16[276,40,1408]{2,1,0:T(8,128)(2,1)} custom-call(s32[40]{0:T(128)} %copy-done.3, f32[40,16,768]{2,1,0:T(8,128)} %pad.22.ph_ref, bf16[16,2,20,40,128]{4,3,2,1,0:T(8,128)(2,1)} %bitcast.35.refs_0_), custom_call_target="tpu_custom_call" | custom-call | flops 5536481280 | bytes 20971520 | tf_op jit(solution)/shard_map/adjoint_dft/pallas_call | solution.py:343
  760.3 62.5 %all-to-all-done.2 = bf16[640,48,128]{2,1,0:T(8,128)(2,1)} async-done(((bf16[640,48,128]{2,1,0:T(8,128)(2,1)}), bf16[640,48,128]{2,1,0:T(8,128)(2,1)}, u32[]{:S(2)}, u32[]{:S(2)}) %all-to-all-start.2) | async-done | bytes 7864352 | tf_op jit(solution)/shard_map/all_to_all | solution.py:404
  822.9 76.5 %adjoint_dft.3 = (bf16[276,40,1408]{2,1,0:T(8,128)(2,1)}, bf16[32,40,1408]{2,1,0:T(8,128)(2,1)}) custom-call(s32[40]{0:T(128)} %copy-done.3, f32[40,16,768]{2,1,0:T(8,128)} %pad.22.ph_ref, bf16[16,2,20,48,128]{4,3,2,1,0:T(8,128)(2,1)} %bitcast.30.refs_0_.refs_1_, ...), custom_call_target="tpu_custom_call", output_to_operand_aliasing={{0}: (4, {})} | custom-call | flops 5536481280 | bytes 20971520 | tf_op jit(solution)/shard_map/adjoint_dft/pallas_call | solution.py:343
  (40 shorter events, 21.4 us)
Async XLA Ops:
  0.6 0.8 copy-start
  2.9 14.6 %copy-start.3 = (s32[40]{0:T(128)}, s32[40]{0:T(128)S(1)}, u32[]{:S(2)}) copy-start(s32[40]{0:T(128)S(1)} %get-tuple-element.23.len_ref) | copy-start | bytes 484
  77.5 154.4 %all-to-all-start = ((bf16[640,40,128]{2,1,0:T(8,128)(2,1)}), bf16[640,40,128]{2,1,0:T(8,128)(2,1)}, u32[]{:S(2)}, u32[]{:S(2)}) async-start(bf16[640,40,128]{2,1,0:T(8,128)(2,1)} %bitcast.152), calls=%async_computation | async-start | bytes 13107200 | tf_op jit(solution)/shard_map/all_to_all | solution.py:404
  232.0 6.8 copy-start.2
  232.0 6.9 copy-start.4
  232.0 181.0 %all-to-all-start.1 = ((bf16[640,48,128]{2,1,0:T(8,128)(2,1)}), bf16[640,48,128]{2,1,0:T(8,128)(2,1)}, u32[]{:S(2)}, u32[]{:S(2)}) async-start(bf16[640,48,128]{2,1,0:T(8,128)(2,1)} %bitcast.150), calls=%async_computation.1 | async-start | bytes 15728640 | tf_op jit(solution)/shard_map/all_to_all | solution.py:404
  412.9 230.1 %all-to-all-start.3 = ((bf16[640,40,128]{2,1,0:T(8,128)(2,1)}), bf16[640,40,128]{2,1,0:T(8,128)(2,1)}, u32[]{:S(2)}, u32[]{:S(2)}) async-start(bf16[640,40,128]{2,1,0:T(8,128)(2,1)} %bitcast.151), calls=%async_computation.3 | async-start | bytes 13107200 | tf_op jit(solution)/shard_map/all_to_all | solution.py:404
  643.1 179.8 %all-to-all-start.2 = ((bf16[640,48,128]{2,1,0:T(8,128)(2,1)}), bf16[640,48,128]{2,1,0:T(8,128)(2,1)}, u32[]{:S(2)}, u32[]{:S(2)}) async-start(bf16[640,48,128]{2,1,0:T(8,128)(2,1)} %bitcast.149), calls=%async_computation.2 | async-start | bytes 15728640 | tf_op jit(solution)/shard_map/all_to_all | solution.py:404
  822.9 79.7 %copy-start.1 = (s32[640]{0:T(1024)S(1)}, s32[640]{0:T(1024)}, u32[]{:S(2)}) copy-start(s32[640]{0:T(1024)} %param.11) | copy-start | bytes 7684

commit v2 on v1

--- a/solution.py
+++ b/solution.py
@@ -8,6 +8,7 @@
 from jax.experimental.pallas import tpu as pltpu
 from jax.sharding import PartitionSpec as P
 
+
 STEPS = 2
 KB = 256
 GROUP = 8
@@ -22,9 +23,13 @@
     exponents = [1 << bit for bit in range(8)] + [KB * block for block in range(block_count)]
     exponents = jnp.asarray(exponents, dtype=jnp.int32)
     length = lengths[:, None, None]
-    phase = (exponents[None, :, None] * wave_ids[None, None, :]) % length
     length_f = length.astype(jnp.float32)
-    turn = phase.astype(jnp.float32) / length_f
+    product = (exponents[None, :, None] * wave_ids[None, None, :]).astype(jnp.float32)
+    inverse = 1.0 / length_f
+    phase = product - jnp.floor(product * inverse) * length_f
+    phase = jnp.where(phase < 0.0, phase + length_f, phase)
+    phase = jnp.where(phase >= length_f, phase - length_f, phase)
+    turn = phase * inverse
     quarter = jnp.floor(turn * 4.0 + 0.5)
     x = (turn - 0.25 * quarter) * jnp.float32(2.0 * math.pi)
     x2 = x * x
@@ -88,7 +93,7 @@
 
 
 def forward_kernel(
-    wave_count, wave_pad, scale_row, groups, rest, len_ref, ph_ref, *refs
+    wave_count, wave_pad, scale_row, first, groups, rest, len_ref, ph_ref, *refs
 ):
     if rest:
         grid_ref, grid_rest_ref, out_ref, base_ref, table_ref, wide_ref, acc_ref, rows_ref, wide_rest_ref, rest_ref = refs
@@ -116,7 +121,7 @@
                 wide_rest_ref[lane] = piece.reshape(rest_cols * GROUP, LANES)
 
         def per_slot(slot, carry):
-            length = len_ref[group * GROUP + slot]
+            length = len_ref[(first + group) * GROUP + slot]
             build_base(ph_ref, base_ref, slot, wave_pad, scale_row)
             acc_ref[...] = jnp.zeros_like(acc_ref)
 
@@ -144,7 +149,7 @@
                     turned[:wave_count]
                 )
                 if rest:
-                    cycle = group * GROUP + slot
+                    cycle = (first + group) * GROUP + slot
                     turned = acc_ref[LANES:, lanes].T[:wave_count]
                     fill = jnp.zeros((wave_count, LANES - rest_cols), jnp.float32)
                     turned = jnp.concatenate([turned, fill], axis=1)
@@ -173,17 +178,17 @@
         run_group()
 
 
-def forward_dft(grid, lengths, phasors, owners, wave_count, wave_pad, scale_row, chunk):
+def forward_dft(grid, lengths, phasors, owners, wave_count, wave_pad, scale_row, chunk, span):
     index, rest, rest_cols, rest_index = chunk
-    col_count, cycle_dev, segment = grid.shape
-    groups = pl.cdiv(cycle_dev, GROUP)
+    _, _, segment = grid.shape
+    first, groups = span[0], span[1] - span[0]
     wide_lanes = round_up(segment, KB) // LANES
     wave_dev = wave_count // owners
     rows = (groups + (1 if rest else 0)) * GROUP
-    last = groups - 1
+    last = span[1] - 1
     in_specs = [
-        pl.BlockSpec((GROUP,) + phasors.shape[1:], lambda g, n: (jnp.minimum(g, last), 0, 0)),
-        pl.BlockSpec((LANES, GROUP, segment), lambda g, n: (index, jnp.minimum(g, last), 0)),
+        pl.BlockSpec((GROUP,) + phasors.shape[1:], lambda g, n: (jnp.minimum(first + g, last), 0, 0)),
+        pl.BlockSpec((LANES, GROUP, segment), lambda g, n: (index, jnp.minimum(first + g, last), 0)),
     ]
     operands = [lengths, phasors, grid]
     scratch = [
@@ -195,7 +200,7 @@
     ]
     if rest:
         in_specs.append(
-            pl.BlockSpec((rest_cols, GROUP, segment), lambda g, n: (rest_index, jnp.minimum(g, last), 0))
+            pl.BlockSpec((rest_cols, GROUP, segment), lambda g, n: (rest_index, jnp.minimum(first + g, last), 0))
         )
         operands.append(grid)
         scratch += [
@@ -203,7 +208,7 @@
             pltpu.VMEM((2 * wave_count * GROUP, LANES), jnp.float32),
         ]
     return pl.pallas_call(
-        functools.partial(forward_kernel, wave_count, wave_pad, scale_row, groups, rest),
+        functools.partial(forward_kernel, wave_count, wave_pad, scale_row, first, groups, rest),
         out_shape=jax.ShapeDtypeStruct((owners, 2, wave_dev, rows, LANES), jnp.bfloat16),
         grid_spec=pltpu.PrefetchScalarGridSpec(
             num_scalar_prefetch=1,
@@ -216,20 +221,19 @@
             dimension_semantics=("arbitrary",), vmem_limit_bytes=56 * 1024 * 1024
         ),
         cost_estimate=pl.CostEstimate(
-            flops=2 * LANES * cycle_dev * segment * wave_pad,
-            bytes_accessed=2 * LANES * cycle_dev * (segment + 2 * wave_count),
+            flops=2 * LANES * groups * GROUP * segment * wave_pad,
+            bytes_accessed=2 * LANES * groups * GROUP * (segment + 2 * wave_count),
             transcendentals=0,
         ),
         name="forward_dft",
     )(*operands)
 
 
-def adjoint_kernel(wave_count, wave_pad, scale_row, rest, aliased, len_ref, ph_ref, *refs):
+def adjoint_kernel(wave_count, wave_pad, scale_row, first, rest, aliased, len_ref, ph_ref, *refs):
     refs = list(refs)
     back_ref = refs.pop(0)
     back_rest_ref = refs.pop(0) if rest else None
-    if aliased:
-        refs.pop(0)
+    del refs[:aliased]
     out_ref = refs.pop(0)
     out_rest_ref = refs.pop(0) if rest else None
     base_ref, table_ref, lhs_ref, rows_ref, wide_ref = refs[:5]
@@ -262,14 +266,14 @@
             wide_rest_ref[lane_block, pl.ds(slot, rest_cols, stride=GROUP), :] = values[LANES:]
 
     def per_slot(slot, carry):
-        length = len_ref[group * GROUP + slot]
+        length = len_ref[(first + group) * GROUP + slot]
         build_base(ph_ref, base_ref, slot, wave_pad, scale_row)
         for part in range(2):
             lanes = slice(part * wave_pad, part * wave_pad + wave_count)
             turned = rows_ref[pl.ds(part * span + slot, wave_count, stride=GROUP), :].T
             lhs_ref[:LANES, lanes] = turned.astype(jnp.bfloat16)
             if rest:
-                cycle = group * GROUP + slot
+                cycle = (first + group) * GROUP + slot
                 rows = rest_ref[pl.ds(part * span + cycle // per_row, wave_count, stride=GROUP), :]
                 rows = pltpu.roll(rows, LANES - lax.rem(cycle, per_row) * rest, 1)
                 lhs_ref[LANES:, lanes] = rows[:, :rest_cols].T.astype(jnp.bfloat16)
@@ -304,20 +308,20 @@
             out_rest_ref[:, :, lanes] = values.astype(jnp.bfloat16)
 
 
-def adjoint_dft(back, field, lengths, phasors, out_shape, wave_count, wave_pad, scale_row, chunk):
-    index, rest, rest_cols, rest_index = chunk
-    col_count, cycle_dev, segment = out_shape
-    owners, _, wave_dev, rows, _ = back.shape
-    groups = pl.cdiv(cycle_dev, GROUP)
+def adjoint_dft(back, back_rest, fields, lengths, phasors, out_shape, wave_count, wave_pad, scale_row, chunk, span):
+    index, rest, rest_cols, _ = chunk
+    _, cycle_dev, segment = out_shape
+    owners, _, wave_dev, _, _ = back.shape
+    first, groups = span[0], span[1] - span[0]
     wide_lanes = round_up(segment, KB) // LANES
-    aliased = field is not None
+    aliased = len(fields)
     block = (owners, 2, wave_dev, GROUP, LANES)
     in_specs = [
-        pl.BlockSpec((GROUP,) + phasors.shape[1:], lambda g, n: (g, 0, 0)),
+        pl.BlockSpec((GROUP,) + phasors.shape[1:], lambda g, n: (first + g, 0, 0)),
         pl.BlockSpec(block, lambda g, n: (0, 0, 0, g, 0)),
     ]
     operands = [lengths, phasors, back]
-    out_specs = [pl.BlockSpec((LANES, GROUP, segment), lambda g, n: (index, g, 0))]
+    out_specs = [pl.BlockSpec((LANES, GROUP, segment), lambda g, n: (index, first + g, 0))]
     out_shapes = [jax.ShapeDtypeStruct(out_shape, jnp.bfloat16)]
     scratch = [
         pltpu.VMEM((KB, 2 * wave_pad), jnp.float32),
@@ -327,21 +331,22 @@
         pltpu.VMEM((wide_lanes, LANES * GROUP, LANES), jnp.float32),
     ]
     if rest:
-        in_specs.append(pl.BlockSpec(block, lambda g, n: (0, 0, 0, groups, 0)))
-        operands.append(back)
-        out_specs.append(pl.BlockSpec((rest_cols, GROUP, segment), lambda g, n: (0, g, 0)))
+        rest_block = back_rest.shape[3] // GROUP - 1
+        in_specs.append(pl.BlockSpec(block, lambda g, n: (0, 0, 0, rest_block, 0)))
+        operands.append(back_rest)
+        out_specs.append(pl.BlockSpec((rest_cols, GROUP, segment), lambda g, n: (0, first + g, 0)))
         out_shapes.append(jax.ShapeDtypeStruct((rest_cols, cycle_dev, segment), jnp.bfloat16))
         scratch += [
             pltpu.VMEM((wide_lanes, rest_cols * GROUP, LANES), jnp.float32),
             pltpu.VMEM((2 * wave_count * GROUP, LANES), jnp.float32),
         ]
     aliases = {}
-    if aliased:
-        aliases = {len(operands): 0}
+    for output, field in enumerate(fields):
+        aliases[len(operands)] = output
         in_specs.append(pl.BlockSpec(memory_space=pl.ANY))
         operands.append(field)
     return pl.pallas_call(
-        functools.partial(adjoint_kernel, wave_count, wave_pad, scale_row, rest, aliased),
+        functools.partial(adjoint_kernel, wave_count, wave_pad, scale_row, first, rest, aliased),
         out_shape=out_shapes,
         grid_spec=pltpu.PrefetchScalarGridSpec(
             num_scalar_prefetch=1, grid=(groups,), in_specs=in_specs, out_specs=out_specs, scratch_shapes=scratch
@@ -351,8 +356,8 @@
             dimension_semantics=("arbitrary",), vmem_limit_bytes=60 * 1024 * 1024
         ),
         cost_estimate=pl.CostEstimate(
-            flops=2 * LANES * cycle_dev * segment * wave_pad,
-            bytes_accessed=2 * LANES * cycle_dev * (segment + 2 * wave_count),
+            flops=2 * LANES * groups * GROUP * segment * wave_pad,
+            bytes_accessed=2 * LANES * groups * GROUP * (segment + 2 * wave_count),
             transcendentals=0,
         ),
         name="adjoint_dft",
@@ -371,10 +376,10 @@
     return chunks
 
 
-def per_device(grid, cycle_ids, cycle_len, wave_ids, legendre, target, step_w, chan_w):
+def device_program(grid, cycle_ids, cycle_len, wave_ids, legendre, target, step_w, chan_w):
     _, batch_size, chan_count, cycle_dev, segment = grid.shape
     wave_count = wave_ids.shape[0]
-    wave_dev, degree_count, cycle_count = legendre.shape
+    wave_dev, degree_count, _ = legendre.shape
     owners = wave_count // wave_dev
     col_count = batch_size * chan_count
     wave_pad = round_up(wave_count, LANES)
@@ -405,11 +410,24 @@
 
     chunks = column_chunks(col_count)
     groups = pl.cdiv(cycle_dev, GROUP)
+    last = len(chunks) - 1
+    head, tail = max(1, groups // 5), max(1, 2 * groups // 5)
+    spans_out = [[(0, groups)] for _ in chunks]
+    spans_back = [[(0, groups)] for _ in chunks]
+    if groups > 1:
+        spans_out[0] = [(0, head), (head, groups)]
+        spans_back[last] = [(0, groups - tail), (groups - tail, groups)]
     sent = []
-    for chunk in chunks:
-        part = forward_dft(grid3, lengths, phasors, owners, wave_count, wave_pad, scale_row, chunk)
-        part, lengths, legendre, target3 = lax.optimization_barrier((part, lengths, legendre, target3))
-        sent.append(part)
+    for number, chunk in enumerate(chunks):
+        parts = []
+        for span in spans_out[number]:
+            rides = chunk if span[1] == groups else (chunk[0], 0, 0, 0)
+            part = forward_dft(
+                grid3, lengths, phasors, owners, wave_count, wave_pad, scale_row, rides, span
+            )
+            part, lengths, legendre, target3 = lax.optimization_barrier((part, lengths, legendre, target3))
+            parts.append(part)
+        sent.append(parts)
     legendre_cols = jnp.take(legendre, cycle_ids, axis=2).reshape(
         wave_dev, degree_count, owners, cycle_dev
     )
@@ -431,15 +449,17 @@
 
     partial_value = jnp.float32(0.0)
     coeff_parts, backs = [], []
-    for chunk, part in zip(chunks, sent):
+    for number, chunk in enumerate(chunks):
         index, rest = chunk[:2]
-        gathered = exchange(part)
+        gathered = [exchange(part) for part in sent[number]]
+        gathered = gathered[0] if len(gathered) == 1 else jnp.concatenate(gathered, axis=3)
         coeff_part, value, back = owner_pass(gathered[:, :, :, :cycle_dev], index * LANES, LANES)
         coeff_parts.append(coeff_part)
         partial_value = partial_value + value
         row_pad = groups * GROUP - cycle_dev
         if row_pad:
             back = jnp.pad(back, ((0, 0),) * 3 + ((0, row_pad), (0, 0)))
+        pieces = [back[:, :, :, span[0] * GROUP : span[1] * GROUP] for span in spans_back[number]]
         if rest:
             per_row = LANES // rest
             lead = gathered.shape[:3]
@@ -451,24 +471,39 @@
             back_rest = jnp.pad(back_rest, ((0, 0),) * 3 + ((0, GROUP * per_row - cycle_dev), (0, 0)))
             back_rest = back_rest.reshape(lead + (GROUP, per_row * rest))
             back_rest = jnp.pad(back_rest, ((0, 0),) * 4 + ((0, LANES - per_row * rest),))
-            back = jnp.concatenate([back, back_rest], axis=3)
-        backs.append(back)
-    loss_sum = lax.psum(partial_value, ("lat", "fld"))
-    backs[-1], loss_sum = lax.optimization_barrier((backs[-1], loss_sum))
-    field = None
-    for chunk, back in zip(chunks, backs):
+            pieces[0] = jnp.concatenate([pieces[0], back_rest], axis=3)
+        backs.append(pieces)
+    coeff_out = jnp.concatenate(coeff_parts, axis=0)
+    coeff_out = coeff_out.reshape(1, batch_size, chan_count, 2, wave_dev, degree_count)
+    fields, loss_sum = [], None
+    steps = [
+        (chunk, part, span, backs[number][part])
+        for number, chunk in enumerate(chunks)
+        for part, span in enumerate(spans_back[number])
+    ]
+    returned_rest = None
+    for number, (chunk, part, span, back) in enumerate(steps):
+        if loss_sum is not None and number == len(steps) - 1:
+            back, loss_sum = lax.optimization_barrier((back, loss_sum))
         returned = exchange(back)
-        results = adjoint_dft(
-            returned, field, lengths, phasors, grid3.shape, wave_count, wave_pad, scale_row, chunk
+        returned_rest = returned if part == 0 else returned_rest
+        fields = list(
+            adjoint_dft(
+                returned, returned_rest, fields, lengths, phasors, grid3.shape, wave_count, wave_pad,
+                scale_row, chunk, span,
+            )
         )
-        field = results[0]
-        if chunk[1]:
-            field = lax.dynamic_update_slice(field, results[1][: chunk[1]], (col_count - chunk[1], 0, 0))
-    coeff_out = jnp.concatenate(coeff_parts, axis=0)
+        if loss_sum is None:
+            fields[0], partial_value = lax.optimization_barrier((fields[0], partial_value))
+            loss_sum = lax.psum(partial_value, ("lat", "fld"))
+    field = fields[0]
+    if chunks[last][1]:
+        rest = chunks[last][1]
+        field = lax.dynamic_update_slice(field, fields[1][:rest], (col_count - rest, 0, 0))
     term_count = STEPS * col_count * wave_count * (wave_count + 1) // 2
     loss = loss_sum / jnp.float32(term_count)
     return (
-        coeff_out.reshape(1, batch_size, chan_count, 2, wave_dev, degree_count),
+        coeff_out,
         loss,
         field.reshape(1, batch_size, chan_count, cycle_dev, segment),
     )
@@ -476,7 +511,7 @@
 
 def solution(mesh):
     return jax.shard_map(
-        per_device,
+        device_program,
         mesh=mesh,
         in_specs=(
             P("fld", None, None, "lat", None),

time: 915 us -> 833 us (0.910)
  blocking collectives: 103 us -> 53.9 us
  waiting for transfers between devices: 203 us -> 161 us
  starting transfers between devices: 26.3 us -> 40.7 us
  other arithmetic: 58.8 us -> 46.4 us
    psum x1, blocking collectives: 103 us -> 53.9 us  [device_program(): loss_sum = lax.psum(partial_value, ('lat', 'fld'))]
    all_to_all x4 -> x6, waiting for transfers between devices: 203 us -> 161 us  [exchange(): lax.all_to_all(flat, 'lat', split_axis=0, concat_axis=0, tiled=True)]
    all_to_all x4 -> x6, starting transfers between devices: 26.3 us -> 40.7 us  [exchange(): lax.all_to_all(flat, 'lat', split_axis=0, concat_axis=0, tiled=True)]
    concatenate x1 -> x2, local copies, waits for them, and re-layouts: 25.6 us -> 29.5 us  [the longest x1 25.6 us: device_program(): coeff_out = jnp.concatenate(coeff_parts, axis=0)]
    pallas_call x2 -> x3, Pallas kernels: 145 us -> 147 us  [adjoint_dft(): pl.pallas_call(functools.partial(adjoint_kernel, wave_count, wave_pad, sc...]
    pallas_call x2 -> x3, Pallas kernels: 132 us -> 134 us  [forward_dft(): pl.pallas_call(functools.partial(forward_kernel, wave_count, wave_pad, sc...]
  transfers between devices with their start and end apart: 4 -> 6, of which waited for: 3 -> 3; matrix products, arithmetic and copies ran while one was open for 30% -> 32% of each run, Pallas kernels for 16% -> 28%
where the time goes in v2:
time: 833 us; the launch traced here: 821 us
  Pallas kernels  280 us (34%)
  waiting for transfers between devices  161 us (19%)
  local copies, waits for them, and re-layouts  159 us (19%)
  matrix products  74.7 us (9%)
  blocking collectives  53.9 us (6%)
  other arithmetic  46.4 us (6%)
  starting transfers between devices  40.7 us (5%)
    all_to_all x6, waiting for transfers between devices, exchange(): lax.all_to_all(flat, 'lat', split_axis=0, concat_axis=0, tiled=True)  161 us
    pallas_call x3, Pallas kernels, adjoint_dft(): pl.pallas_call(functools.partial(adjoint_kernel, wave_count, wave_pad, sc...  147 us
    pallas_call x3, Pallas kernels, forward_dft(): pl.pallas_call(functools.partial(forward_kernel, wave_count, wave_pad, sc...  134 us
    psum x1, blocking collectives, device_program(): loss_sum = lax.psum(partial_value, ('lat', 'fld'))  53.9 us
    optimization_barrier x2, local copies, waits for them, and re-layouts, device_program(): lax.optimization_barrier((part, lengths, legendre, target3))  41.2 us
    all_to_all x6, starting transfers between devices, exchange(): lax.all_to_all(flat, 'lat', split_axis=0, concat_axis=0, tiled=True)  40.7 us
    dot_general x3, matrix products, owner_pass(): jnp.einsum('sndp,sntc->dtspc', legendre_cols, grad_coeff, preferred_eleme...  39.2 us
    dot_general x3, matrix products, owner_pass(): jnp.einsum('sndp,dtspc->sntc', legendre_cols, gathered, preferred_element...  35.6 us
  transfers between devices with their start and end apart: 6, of which 3 were waited for; matrix products, arithmetic and copies ran while one was open for 32% of the time, Pallas kernels for 28%

profile of v2, /device:TPU:28, one launch (start us, length us, event | category | flops | bytes accessed | tf_op | source)
XLA Modules:
  0.0 820.8 jit_solution(5287574303522282753)
XLA Ops:
  8.3 14.0 %forward_dft.3 = bf16[16,2,20,8,128]{4,3,2,1,0:T(8,128)(2,1)} custom-call(s32[40]{0:T(128)} %copy-done.3, f32[40,16,768]{2,1,0:T(8,128)} %pad.22.ph_ref, bf16[276,40,1408]{2,1,0:T(8,128)(2,1)} %bitcast.148), custom_call_target="tpu_custom_call" | custom-call | flops 1107296256 | bytes 4194304 | tf_op jit(solution)/shard_map/forward_dft/pallas_call | solution.py:210
  22.4 7.8 all-to-all-start
  30.2 48.3 %forward_dft.4 = bf16[16,2,20,32,128]{4,3,2,1,0:T(8,128)(2,1)} custom-call(s32[40]{0:T(128)} %copy-done.3, f32[40,16,768]{2,1,0:T(8,128)} %pad.22.ph_ref, bf16[276,40,1408]{2,1,0:T(8,128)(2,1)} %bitcast.149), custom_call_target="tpu_custom_call" | custom-call | flops 4429185024 | bytes 16777216 | tf_op jit(solution)/shard_map/forward_dft/pallas_call | solution.py:210
  78.5 7.0 all-to-all-start.1
  85.4 71.2 %forward_dft.5 = bf16[16,2,20,48,128]{4,3,2,1,0:T(8,128)(2,1)} custom-call(s32[40]{0:T(128)} %copy-done.3, f32[40,16,768]{2,1,0:T(8,128)} %pad.22.ph_ref, bf16[276,40,1408]{2,1,0:T(8,128)(2,1)} %bitcast.150, bf16[276,40,1408]{2,1,0:T(8,128)(2,1)} %bitcast.151), custom_call_target="tpu_custom_call" | custom-call | flops 5536481280 | bytes 20971520 | tf_op jit(solution)/shard_map/forward_dft/pallas_call | solution.py:210
  156.7 44.6 %all-to-all-done.1 = bf16[640,32,128]{2,1,0:T(8,128)(2,1)} async-done(((bf16[640,32,128]{2,1,0:T(8,128)(2,1)}), bf16[640,32,128]{2,1,0:T(8,128)(2,1)}, u32[]{:S(2)}, u32[]{:S(2)}) %all-to-all-start.1) | async-done | bytes 5242912 | tf_op jit(solution)/shard_map/all_to_all | solution.py:409
  201.3 7.0 all-to-all-start.2
  209.2 15.0 %copy.22 = bf16[20,320,640]{1,0,2:T(8,128)(2,1)} copy(bf16[20,320,640]{2,1,0:T(8,128)(2,1)} %param.13) | data formatting | bytes 16384000 | tf_op jit(solution)/shard_map/optimization_barrier | solution.py:428
  224.2 25.5 %gather_fusion.1 = bf16[640,20,320]{2,1,0:T(8,128)(2,1)} fusion(bf16[20,320,640]{1,0,2:T(8,128)(2,1)} %copy.22, s32[1024]{0:T(1024)S(1)} %pad_clamp_fusion), kind=kCustom, calls=%fused_computation.1 | custom fusion | bytes 16386560 | tf_op jit(solution)/shard_map/jit(_take)/gather | solution.py:431
  249.7 9.9 %copy.23 = bf16[20,320,640]{1,2,0:T(8,128)(2,1)} copy(bf16[20,320,640]{1,0,2:T(8,128)(2,1)} %bitcast.153) | data formatting | bytes 16384000 | tf_op jit(solution)/shard_map/jit(_take)/gather | solution.py:431
  259.6 26.2 %copy.30 = f32[276,2,20,320]{0,3,1,2:T(8,128)} copy(f32[276,2,20,320]{3,1,2,0:T(2,128)} %bitcast.158) | data formatting | bytes 28262400 | tf_op jit(solution)/shard_map/optimization_barrier | solution.py:428
  286.7 11.7 %fusion.11 = f32[20,320,2,128,1]{3,1,4,2,0:T(8,128)} fusion(bf16[20,320,16,40]{1,3,2,0:T(8,128)(2,1)} %bitcast.162, pred[16,40]{1,0:T(8,128)(4,1)S(1)} %broadcast_in_dim.62, bf16[16,2,20,32,128]{4,3,2,1,0:T(8,128)(2,1)} %bitcast.9, bf16[16,2,20,8,128]{4,3,2,1,0:T(8,128)(2,1)S(1)} %bitcast.169), kind=kOutput, calls=%fused_computation.15 | convolution fusion | flops 2114355200 | bytes 21299840 | tf_op jit(solution)/shard_map/sndp,dtspc->sntc/dot_general | solution.py:436
  298.5 11.9 %fusion.34 = bf16[16,2,20,40,128]{4,3,0,1,2:T(8,128)(2,1)} fusion(bf16[20,320,16,40]{1,3,2,0:T(8,128)(2,1)} %bitcast.163, pred[16,40]{1,0:T(8,128)(4,1)S(1)} %broadcast_in_dim.62, f32[20,128]{1,0:T(8,128)S(1)} %get-tuple-element.63, f32[276,2,20,320]{0,3,1,2:T(8,128)} %copy.30, f32[20,320,2,128,1]{3,1,4,2,0:T(8,128)} %fusion.11, f32[20,320]{1,0:T(8,128)S(1)} %fusion.65), kind=kOutput, calls=%fused_computation.48 | convolution fusion | flops 2112716800 | bytes 29527680 | tf_op jit(solution)/shard_map/sndp,sntc->dtspc/dot_general | solution.py:445
  310.4 7.2 copy.32
  317.6 67.0 %all-to-all-done.2 = bf16[640,48,128]{2,1,0:T(8,128)(2,1)} async-done(((bf16[640,48,128]{2,1,0:T(8,128)(2,1)}), bf16[640,48,128]{2,1,0:T(8,128)(2,1)}, u32[]{:S(2)}, u32[]{:S(2)}) %all-to-all-start.2) | async-done | bytes 7864352 | tf_op jit(solution)/shard_map/all_to_all | solution.py:409
  392.5 7.0 reshape.379
  399.5 11.9 %fusion.7 = f32[20,320,2,20,1]{3,1,4,2,0:T(8,128)} fusion(bf16[20,320,16,40]{1,3,2,0:T(8,128)(2,1)} %bitcast.164, pred[16,40]{1,0:T(8,128)(4,1)S(1)} %broadcast_in_dim.62, bf16[16,2,20,48,20]{4,3,2,1,0:T(8,128)(2,1)} %reshape.379), kind=kOutput, calls=%fused_computation.11 | convolution fusion | flops 331776000 | bytes 17408640 | tf_op jit(solution)/shard_map/sndp,dtspc->sntc/dot_general | solution.py:436
  411.4 15.3 %convert_bitcast_fusion = bf16[16,2,20,40,20]{3,4,0,1,2:T(8,128)(2,1)} fusion(bf16[20,320,16,40]{1,3,2,0:T(8,128)(2,1)} %bitcast.165, pred[16,40]{1,0:T(8,128)(4,1)S(1)} %broadcast_in_dim.62, f32[20,20]{1,0:T(8,128)S(1)} %get-tuple-element.60, f32[276,2,20,320]{0,3,1,2:T(8,128)} %copy.30, f32[20,320,2,20,1]{3,1,4,2,0:T(8,128)} %fusion.7, ...), kind=kOutput, calls=%fused_computation.51 | convolution fusion | flops 333568000 | bytes 23989440 | tf_op jit(solution)/shard_map/sndp,sntc->dtspc/dot_general | solution.py:445
  426.7 8.6 %copy.54 = bf16[16,2,20,40,20]{4,3,0,1,2:T(8,128)(2,1)} copy(bf16[16,2,20,40,20]{3,4,0,1,2:T(8,128)(2,1)} %convert_bitcast_fusion) | data formatting | bytes 2048000
  435.3 8.0 pad.23.clone
  443.3 9.0 %reshape.415 = bf16[16,2,20,8,120]{4,3,0,1,2:T(8,128)(2,1)S(1)} reshape(bf16[16,2,20,48,20]{4,3,0,1,2:T(8,128)(2,1)} %pad.23.clone) | data formatting | bytes 2457600 | tf_op jit(solution)/shard_map/reshape | solution.py:472
  452.3 11.9 %fusion.9 = f32[20,320,2,128,1]{3,1,4,2,0:T(8,128)} fusion(bf16[20,320,16,40]{1,3,2,0:T(8,128)(2,1)} %bitcast.166, pred[16,40]{1,0:T(8,128)(4,1)S(1)} %broadcast_in_dim.62, bf16[16,2,20,48,128]{4,3,2,1,0:T(8,128)(2,1)} %bitcast.15), kind=kOutput, calls=%fused_computation.13 | convolution fusion | flops 2101248000 | bytes 22938240 | tf_op jit(solution)/shard_map/sndp,dtspc->sntc/dot_general | solution.py:436
  464.2 12.0 %fusion.37 = bf16[16,2,20,40,128]{4,3,0,1,2:T(8,128)(2,1)} fusion(bf16[20,320,16,40]{1,3,2,0:T(8,128)(2,1)} %bitcast.167, pred[16,40]{1,0:T(8,128)(4,1)S(1)} %broadcast_in_dim.62, f32[20,128]{1,0:T(8,128)S(1)} %get-tuple-element.66, f32[276,2,20,320]{0,3,1,2:T(8,128)} %copy.30, f32[20,320,2,128,1]{3,1,4,2,0:T(8,128)} %fusion.9, f32[20,320]{1,0:T(8,128)S(1)} %fusion.65), kind=kOutput, calls=%fused_computation.49 | convolution fusion | flops 2112716800 | bytes 29527680 | tf_op jit(solution)/shard_map/sndp,sntc->dtspc/dot_general | solution.py:445
  483.5 49.1 %all-to-all-done.3 = bf16[640,40,128]{2,1,0:T(8,128)(2,1)} async-done(((bf16[640,40,128]{2,1,0:T(8,128)(2,1)}), bf16[640,40,128]{2,1,0:T(8,128)(2,1)}, u32[]{:S(2)}, u32[]{:S(2)}) %all-to-all-start.3) | async-done | bytes 6553632 | tf_op jit(solution)/shard_map/all_to_all | solution.py:409
  539.2 15.3 %fusion.20 = (f32[]{:T(128)}, f32[]{:T(128)}, f32[128,2,20,320]{0,3,1,2:T(8,128)}, f32[128,2,20,320]{0,3,1,2:T(8,128)}) fusion(f32[20,128]{1,0:T(8,128)S(1)} %get-tuple-element.67, f32[276,2,20,320]{0,3,1,2:T(8,128)} %copy.30, f32[20,320]{1,0:T(8,128)S(1)} %fusion.65, f32[20,320,2,128,1]{3,1,4,2,0:T(8,128)} %fusion.9, f32[20,320,2,128,1]{3,1,4,2,0:T(8,128)} %fusion.11, ...), kind=kLoop, calls=%fused_computation.24 | loop fusion | flops 19660800 | bytes 39367688 | tf_op jit(solution)/shard_map/reduce_sum | solution.py:443
  555.8 8.3 %fusion.21 = (f32[]{:T(128)}, f32[20,2,20,320]{0,3,1,2:T(8,128)}) fusion(f32[20,20]{1,0:T(8,128)S(1)} %get-tuple-element.61, f32[276,2,20,320]{0,3,1,2:T(8,128)} %copy.30, f32[20,320]{1,0:T(8,128)S(1)} %fusion.65, f32[20,320,2,20,1]{3,1,4,2,0:T(8,128)} %fusion.7), kind=kLoop, calls=%fused_computation.25 | loop fusion | flops 1535999 | bytes 3099204 | tf_op jit(solution)/shard_map/reduce_sum | solution.py:443
  564.8 66.9 %adjoint_dft.3.refs_2_ = bf16[276,40,1408]{2,1,0:T(8,128)(2,1)} custom-call(s32[40]{0:T(128)} %copy-done.3, f32[40,16,768]{2,1,0:T(8,128)} %pad.22.ph_ref, bf16[16,2,20,40,128]{4,3,2,1,0:T(8,128)(2,1)} %bitcast.32.refs_0_), custom_call_target="tpu_custom_call" | custom-call | flops 5536481280 | bytes 20971520 | tf_op jit(solution)/shard_map/adjoint_dft/pallas_call | solution.py:348
  631.7 53.9 %psum.7 = f32[]{:T(128)} all-reduce(f32[]{:T(128)S(6)} %add.128), channel_id=1, replica_groups=mesh['lat'=16,'fld'=2] {'lat','fld'}, use_global_device_ids=true, to_apply=%region_3.4 | all-reduce | flops 1 | bytes 8 | tf_op jit(solution)/shard_map/psum | solution.py:498
  693.8 15.1 %pad_maximum_fusion = f32[276,2,20,320]{0,3,1,2:T(8,128)} fusion(f32[20,2,20,320]{0,3,1,2:T(8,128)} %get-tuple-element.53, f32[128,2,20,320]{0,3,1,2:T(8,128)} %get-tuple-element.54, f32[128,2,20,320]{0,3,1,2:T(8,128)} %get-tuple-element.55), kind=kLoop, calls=%fused_computation.2 | loop fusion | flops 7065600 | bytes 28262400 | tf_op jit(solution)/shard_map/concatenate | solution.py:476
  708.9 25.6 %copy.29 = f32[276,2,20,320]{3,1,2,0:T(2,128)} copy(f32[276,2,20,320]{0,3,1,2:T(8,128)} %pad_maximum_fusion) | data formatting | bytes 28262400 | tf_op jit(solution)/shard_map/concatenate | solution.py:476
  735.1 46.2 %adjoint_dft.4 = (bf16[276,40,1408]{2,1,0:T(8,128)(2,1)}, bf16[32,40,1408]{2,1,0:T(8,128)(2,1)}) custom-call(s32[40]{0:T(128)} %copy-done.3, f32[40,16,768]{2,1,0:T(8,128)} %pad.22.ph_ref, bf16[16,2,20,32,128]{4,3,2,1,0:T(8,128)(2,1)} %bitcast.39.refs_0_.refs_1_, ...), custom_call_target="tpu_custom_call", output_to_operand_aliasing={{0}: (4, {})} | custom-call | flops 3321888768 | bytes 12582912 | tf_op jit(solution)/shard_map/adjoint_dft/pallas_call | solution.py:348
  782.8 33.5 %adjoint_dft.5 = (bf16[276,40,1408]{2,1,0:T(8,128)(2,1)}, bf16[32,40,1408]{2,1,0:T(8,128)(2,1)}) custom-call(s32[40]{0:T(128)} %copy-done.3, f32[40,16,768]{2,1,0:T(8,128)} %pad.22.ph_ref, bf16[16,2,20,16,128]{4,3,2,1,0:T(8,128)(2,1)} %bitcast.160, ...), custom_call_target="tpu_custom_call", output_to_operand_aliasing={{0}: (4, {}), {1}: (5, {})} | custom-call | flops 2214592512 | bytes 8388608 | tf_op jit(solution)/shard_map/adjoint_dft/pallas_call | solution.py:348
  (53 shorter events, 43.4 us)
Async XLA Ops:
  0.6 0.8 copy-start
  2.9 5.4 copy-start.3
  22.4 56.1 %all-to-all-start = ((bf16[640,8,128]{2,1,0:T(8,128)(2,1)}), bf16[640,8,128]{2,1,0:T(8,128)(2,1)S(1)}, u32[]{:S(2)}, u32[]{:S(2)}) async-start(bf16[640,8,128]{2,1,0:T(8,128)(2,1)} %bitcast.168), calls=%async_computation | async-start | bytes 2621440 | tf_op jit(solution)/shard_map/all_to_all | solution.py:409
  78.5 122.8 %all-to-all-start.1 = ((bf16[640,32,128]{2,1,0:T(8,128)(2,1)}), bf16[640,32,128]{2,1,0:T(8,128)(2,1)}, u32[]{:S(2)}, u32[]{:S(2)}) async-start(bf16[640,32,128]{2,1,0:T(8,128)(2,1)} %bitcast.157), calls=%async_computation.1 | async-start | bytes 10485760 | tf_op jit(solution)/shard_map/all_to_all | solution.py:409
  201.3 7.6 copy-start.4
  201.3 7.7 copy-start.5
  201.3 183.2 %all-to-all-start.2 = ((bf16[640,48,128]{2,1,0:T(8,128)(2,1)}), bf16[640,48,128]{2,1,0:T(8,128)(2,1)}, u32[]{:S(2)}, u32[]{:S(2)}) async-start(bf16[640,48,128]{2,1,0:T(8,128)(2,1)} %bitcast.154), calls=%async_computation.2 | async-start | bytes 15728640 | tf_op jit(solution)/shard_map/all_to_all | solution.py:409
  384.6 148.0 %all-to-all-start.3 = ((bf16[640,40,128]{2,1,0:T(8,128)(2,1)}), bf16[640,40,128]{2,1,0:T(8,128)(2,1)}, u32[]{:S(2)}, u32[]{:S(2)}) async-start(bf16[640,40,128]{2,1,0:T(8,128)(2,1)} %bitcast.155), calls=%async_computation.3 | async-start | bytes 13107200 | tf_op jit(solution)/shard_map/all_to_all | solution.py:409
  476.2 2.1 slice-start
  532.6 155.1 %all-to-all-start.5 = ((bf16[640,32,128]{2,1,0:T(8,128)(2,1)}), bf16[640,32,128]{2,1,0:T(8,128)(2,1)}, u32[]{:S(2)}, u32[]{:S(2)}) async-start(bf16[640,32,128]{2,1,0:T(8,128)(2,1)} %bitcast.156), calls=%async_computation.5 | async-start | bytes 10485760 | tf_op jit(solution)/shard_map/all_to_all | solution.py:409
  564.8 120.8 %slice-start.1 = ((bf16[16,2,20,40,128]{4,3,0,1,2:T(8,128)(2,1)}), bf16[16,2,20,16,128]{4,3,0,1,2:T(8,128)(2,1)S(1)}, s32[]{:S(2)}) async-start(bf16[16,2,20,40,128]{4,3,0,1,2:T(8,128)(2,1)} %fusion.37), calls=%async_computation.7 | async-start | bytes 5242880 | tf_op jit(solution)/shard_map/slice | solution.py:462
  687.7 93.6 %all-to-all-start.4 = ((bf16[640,16,128]{2,1,0:T(8,128)(2,1)}), bf16[640,16,128]{2,1,0:T(8,128)(2,1)S(1)}, u32[]{:S(2)}, u32[]{:S(2)}) async-start(bf16[640,16,128]{2,1,0:T(8,128)(2,1)} %bitcast.161), calls=%async_computation.4 | async-start | bytes 5242880 | tf_op jit(solution)/shard_map/all_to_all | solution.py:409
  781.3 1.5 copy-start.2
  782.8 36.7 %copy-start.1 = (s32[640]{0:T(1024)S(1)}, s32[640]{0:T(1024)}, u32[]{:S(2)}) copy-start(s32[640]{0:T(1024)} %param.11) | copy-start | bytes 7684

commit v3 on v2

--- a/solution.py
+++ b/solution.py
@@ -13,6 +13,7 @@
 KB = 256
 GROUP = 8
 LANES = 128
+SPLIT = 3
 
 
 def round_up(value, unit):
@@ -364,6 +365,23 @@
     )(*operands)
 
 
+def split_terms(value):
+    terms = []
+    for _ in range(SPLIT):
+        term = lax.reduce_precision(value, exponent_bits=8, mantissa_bits=7)
+        terms.append(term.astype(jnp.bfloat16))
+        value = value - term
+    return terms
+
+
+def place_terms(rows, terms, lane):
+    at = [lax.broadcasted_iota(jnp.int32, rows.shape, axis) for axis in range(1, rows.ndim)]
+    first = (at[0] == 0) & (at[1] == 0) & (at[2] == 0)
+    for number, term in enumerate(terms):
+        rows = jnp.where(first & (at[3] == lane + number), term, rows)
+    return rows
+
+
 def column_chunks(col_count):
     whole = col_count // LANES
     rest = col_count - whole * LANES
@@ -411,7 +429,7 @@
     chunks = column_chunks(col_count)
     groups = pl.cdiv(cycle_dev, GROUP)
     last = len(chunks) - 1
-    head, tail = max(1, groups // 5), max(1, 2 * groups // 5)
+    head = tail = max(1, 2 * groups // 5)
     spans_out = [[(0, groups)] for _ in chunks]
     spans_back = [[(0, groups)] for _ in chunks]
     if groups > 1:
@@ -448,6 +466,7 @@
         return jnp.transpose(coeffs, (3, 2, 0, 1)), value, back
 
     partial_value = jnp.float32(0.0)
+    loss_lane = None
     coeff_parts, backs = [], []
     for number, chunk in enumerate(chunks):
         index, rest = chunk[:2]
@@ -470,32 +489,39 @@
             partial_value = partial_value + value
             back_rest = jnp.pad(back_rest, ((0, 0),) * 3 + ((0, GROUP * per_row - cycle_dev), (0, 0)))
             back_rest = back_rest.reshape(lead + (GROUP, per_row * rest))
-            back_rest = jnp.pad(back_rest, ((0, 0),) * 4 + ((0, LANES - per_row * rest),))
+            spare = LANES - per_row * rest
+            back_rest = jnp.pad(back_rest, ((0, 0),) * 4 + ((0, spare),))
+            if number == last and spare >= SPLIT:
+                loss_lane = per_row * rest
+                back_rest = place_terms(back_rest, split_terms(partial_value), loss_lane)
             pieces[0] = jnp.concatenate([pieces[0], back_rest], axis=3)
         backs.append(pieces)
     coeff_out = jnp.concatenate(coeff_parts, axis=0)
     coeff_out = coeff_out.reshape(1, batch_size, chan_count, 2, wave_dev, degree_count)
-    fields, loss_sum = [], None
+    fields = []
     steps = [
         (chunk, part, span, backs[number][part])
         for number, chunk in enumerate(chunks)
         for part, span in enumerate(spans_back[number])
     ]
     returned_rest = None
-    for number, (chunk, part, span, back) in enumerate(steps):
-        if loss_sum is not None and number == len(steps) - 1:
-            back, loss_sum = lax.optimization_barrier((back, loss_sum))
+    for chunk, part, span, back in steps:
         returned = exchange(back)
         returned_rest = returned if part == 0 else returned_rest
+        if loss_lane is not None and chunk[1] and part == 0:
+            row = returned.shape[3] - GROUP
+            terms = returned[:, 0, 0, row, loss_lane : loss_lane + SPLIT]
+            partial_value = jnp.sum(terms.astype(jnp.float32))
         fields = list(
             adjoint_dft(
                 returned, returned_rest, fields, lengths, phasors, grid3.shape, wave_count, wave_pad,
                 scale_row, chunk, span,
             )
         )
-        if loss_sum is None:
+        if chunk is chunks[last] and part == 0:
             fields[0], partial_value = lax.optimization_barrier((fields[0], partial_value))
-            loss_sum = lax.psum(partial_value, ("lat", "fld"))
+            loss_sum = lax.psum(partial_value, "fld" if loss_lane is not None else ("lat", "fld"))
+            fields[0], loss_sum = lax.optimization_barrier((fields[0], loss_sum))
     field = fields[0]
     if chunks[last][1]:
         rest = chunks[last][1]

time: 833 us -> 865 us (1.038)
  waiting for transfers between devices: 161 us -> 235 us
  blocking collectives: 53.9 us -> 3.08 us
    all_to_all x6, waiting for transfers between devices: 161 us -> 235 us  [exchange(): lax.all_to_all(flat, 'lat', split_axis=0, concat_axis=0, tiled=True)]
    psum x1, blocking collectives: 53.9 us -> 3.08 us  [device_program(): lax.psum(partial_value, 'fld' if loss_lane is not None else ('lat', 'fld'))]
  transfers between devices with their start and end apart: 6 -> 6, of which waited for: 3 -> 5; matrix products, arithmetic and copies ran while one was open for 32% -> 32% of each run, Pallas kernels for 28% -> 26%
where the time goes in v3:
time: 865 us; the launch traced here: 850 us
  Pallas kernels  280 us (32%)
  waiting for transfers between devices  235 us (27%)
  local copies, waits for them, and re-layouts  156 us (18%)
  matrix products  75.1 us (9%)
  other arithmetic  50 us (6%)
  starting transfers between devices  40.4 us (5%)
  between operations  9.64 us (1%)
    all_to_all x6, waiting for transfers between devices, exchange(): lax.all_to_all(flat, 'lat', split_axis=0, concat_axis=0, tiled=True)  235 us
    pallas_call x3, Pallas kernels, adjoint_dft(): pl.pallas_call(functools.partial(adjoint_kernel, wave_count, wave_pad, sc...  147 us
    pallas_call x3, Pallas kernels, forward_dft(): pl.pallas_call(functools.partial(forward_kernel, wave_count, wave_pad, sc...  134 us
    optimization_barrier x2, local copies, waits for them, and re-layouts, device_program(): lax.optimization_barrier((part, lengths, legendre, target3))  41.2 us
    all_to_all x6, starting transfers between devices, exchange(): lax.all_to_all(flat, 'lat', split_axis=0, concat_axis=0, tiled=True)  40.4 us
    dot_general x3, matrix products, owner_pass(): jnp.einsum('sndp,sntc->dtspc', legendre_cols, grad_coeff, preferred_eleme...  39.9 us
    gather x2, local copies, waits for them, and re-layouts, device_program(): jnp.take(legendre, cycle_ids, axis=2)  35.4 us
    dot_general x3, matrix products, owner_pass(): jnp.einsum('sndp,dtspc->sntc', legendre_cols, gathered, preferred_element...  35.3 us
  transfers between devices with their start and end apart: 6, of which 5 were waited for; matrix products, arithmetic and copies ran while one was open for 32% of the time, Pallas kernels for 26%

profile of v3, /device:TPU:28, one launch (start us, length us, event | category | flops | bytes accessed | tf_op | source)
XLA Modules:
  0.0 849.6 jit_solution(5957381353892959948)
XLA Ops:
  8.3 25.4 %forward_dft.3 = bf16[16,2,20,16,128]{4,3,2,1,0:T(8,128)(2,1)} custom-call(s32[40]{0:T(128)} %copy-done.3, f32[40,16,768]{2,1,0:T(8,128)} %pad.22.ph_ref, bf16[276,40,1408]{2,1,0:T(8,128)(2,1)} %bitcast.148), custom_call_target="tpu_custom_call" | custom-call | flops 2214592512 | bytes 8388608 | tf_op jit(solution)/shard_map/forward_dft/pallas_call | solution.py:211
  33.7 8.1 all-to-all-start
  41.8 37.0 %forward_dft.4 = bf16[16,2,20,24,128]{4,3,2,1,0:T(8,128)(2,1)} custom-call(s32[40]{0:T(128)} %copy-done.3, f32[40,16,768]{2,1,0:T(8,128)} %pad.22.ph_ref, bf16[276,40,1408]{2,1,0:T(8,128)(2,1)} %bitcast.149), custom_call_target="tpu_custom_call" | custom-call | flops 3321888768 | bytes 12582912 | tf_op jit(solution)/shard_map/forward_dft/pallas_call | solution.py:211
  78.8 21.2 %all-to-all-done = bf16[640,16,128]{2,1,0:T(8,128)(2,1)S(1)} async-done(((bf16[640,16,128]{2,1,0:T(8,128)(2,1)}), bf16[640,16,128]{2,1,0:T(8,128)(2,1)S(1)}, u32[]{:S(2)}, u32[]{:S(2)}) %all-to-all-start) | async-done | bytes 2621472 | tf_op jit(solution)/shard_map/all_to_all | solution.py:427
  106.2 71.3 %forward_dft.5 = bf16[16,2,20,48,128]{4,3,2,1,0:T(8,128)(2,1)} custom-call(s32[40]{0:T(128)} %copy-done.3, f32[40,16,768]{2,1,0:T(8,128)} %pad.22.ph_ref, bf16[276,40,1408]{2,1,0:T(8,128)(2,1)} %bitcast.150, bf16[276,40,1408]{2,1,0:T(8,128)(2,1)} %bitcast.151), custom_call_target="tpu_custom_call" | custom-call | flops 5536481280 | bytes 20971520 | tf_op jit(solution)/shard_map/forward_dft/pallas_call | solution.py:211
  177.5 14.3 %all-to-all-done.1 = bf16[640,24,128]{2,1,0:T(8,128)(2,1)} async-done(((bf16[640,24,128]{2,1,0:T(8,128)(2,1)}), bf16[640,24,128]{2,1,0:T(8,128)(2,1)}, u32[]{:S(2)}, u32[]{:S(2)}) %all-to-all-start.1) | async-done | bytes 3932192 | tf_op jit(solution)/shard_map/all_to_all | solution.py:427
  191.8 7.4 all-to-all-start.2
  200.1 15.0 %copy.22 = bf16[20,320,640]{1,0,2:T(8,128)(2,1)} copy(bf16[20,320,640]{2,1,0:T(8,128)(2,1)} %param.13) | data formatting | bytes 16384000 | tf_op jit(solution)/shard_map/optimization_barrier | solution.py:446
  215.0 25.5 %gather_fusion.1 = bf16[640,20,320]{2,1,0:T(8,128)(2,1)} fusion(bf16[20,320,640]{1,0,2:T(8,128)(2,1)} %copy.22, s32[1024]{0:T(1024)S(1)} %pad_clamp_fusion), kind=kCustom, calls=%fused_computation.1 | custom fusion | bytes 16386560 | tf_op jit(solution)/shard_map/jit(_take)/gather | solution.py:449
  240.6 9.9 %copy.23 = bf16[20,320,640]{1,2,0:T(8,128)(2,1)} copy(bf16[20,320,640]{1,0,2:T(8,128)(2,1)} %bitcast.153) | data formatting | bytes 16384000 | tf_op jit(solution)/shard_map/jit(_take)/gather | solution.py:449
  250.5 26.2 %copy.30 = f32[276,2,20,320]{0,3,1,2:T(8,128)} copy(f32[276,2,20,320]{3,1,2,0:T(2,128)} %bitcast.157) | data formatting | bytes 28262400 | tf_op jit(solution)/shard_map/optimization_barrier | solution.py:446
  277.6 11.4 %fusion.10 = f32[20,320,2,128,1]{3,1,4,2,0:T(8,128)} fusion(bf16[20,320,16,40]{1,3,2,0:T(8,128)(2,1)} %bitcast.163, pred[16,40]{1,0:T(8,128)(4,1)S(1)} %broadcast_in_dim.72, bf16[16,2,20,24,128]{4,3,2,1,0:T(8,128)(2,1)} %bitcast.9, bf16[16,2,20,16,128]{4,3,2,1,0:T(8,128)(2,1)S(1)} %bitcast.169), kind=kOutput, calls=%fused_computation.13 | convolution fusion | flops 2114355200 | bytes 21299840 | tf_op jit(solution)/shard_map/sndp,dtspc->sntc/dot_general | solution.py:454
  289.1 12.0 %fusion.33 = bf16[16,2,20,40,128]{4,3,0,1,2:T(8,128)(2,1)} fusion(bf16[20,320,16,40]{1,3,2,0:T(8,128)(2,1)} %bitcast.164, pred[16,40]{1,0:T(8,128)(4,1)S(1)} %broadcast_in_dim.72, f32[20,128]{1,0:T(8,128)S(1)} %get-tuple-element.60, f32[276,2,20,320]{0,3,1,2:T(8,128)} %copy.30, f32[20,320,2,128,1]{3,1,4,2,0:T(8,128)} %fusion.10, f32[20,320]{1,0:T(8,128)S(1)} %fusion.63), kind=kOutput, calls=%fused_computation.46 | convolution fusion | flops 2112716800 | bytes 29527680 | tf_op jit(solution)/shard_map/sndp,sntc->dtspc/dot_general | solution.py:463
  301.0 7.3 copy.37
  308.3 67.2 %all-to-all-done.2 = bf16[640,48,128]{2,1,0:T(8,128)(2,1)} async-done(((bf16[640,48,128]{2,1,0:T(8,128)(2,1)}), bf16[640,48,128]{2,1,0:T(8,128)(2,1)}, u32[]{:S(2)}, u32[]{:S(2)}) %all-to-all-start.2) | async-done | bytes 7864352 | tf_op jit(solution)/shard_map/all_to_all | solution.py:427
  383.4 7.0 reshape.380
  390.4 11.9 %fusion.8 = f32[20,320,2,128,1]{3,1,4,2,0:T(8,128)} fusion(bf16[20,320,16,40]{1,3,2,0:T(8,128)(2,1)} %bitcast.165, pred[16,40]{1,0:T(8,128)(4,1)S(1)} %broadcast_in_dim.72, bf16[16,2,20,48,128]{4,3,2,1,0:T(8,128)(2,1)} %bitcast.15), kind=kOutput, calls=%fused_computation.11 | convolution fusion | flops 2101248000 | bytes 22938240 | tf_op jit(solution)/shard_map/sndp,dtspc->sntc/dot_general | solution.py:454
  402.3 15.4 %fusion.19 = (f32[]{:T(128)}, f32[]{:T(128)}, f32[128,2,20,320]{0,3,1,2:T(8,128)}, f32[128,2,20,320]{0,3,1,2:T(8,128)}) fusion(f32[20,128]{1,0:T(8,128)S(1)} %get-tuple-element.66, f32[276,2,20,320]{0,3,1,2:T(8,128)} %copy.30, f32[20,320]{1,0:T(8,128)S(1)} %fusion.63, f32[20,320,2,128,1]{3,1,4,2,0:T(8,128)} %fusion.8, f32[20,320,2,128,1]{3,1,4,2,0:T(8,128)} %fusion.10, ...), kind=kLoop, calls=%fused_computation.22 | loop fusion | flops 19660800 | bytes 39367688 | tf_op jit(solution)/shard_map/reduce_sum | solution.py:461
  419.1 11.9 %fusion.6 = f32[20,320,2,20,1]{3,1,4,2,0:T(8,128)} fusion(bf16[20,320,16,40]{1,3,2,0:T(8,128)(2,1)} %bitcast.166, pred[16,40]{1,0:T(8,128)(4,1)S(1)} %broadcast_in_dim.72, bf16[16,2,20,48,20]{4,3,2,1,0:T(8,128)(2,1)} %reshape.380), kind=kOutput, calls=%fused_computation.9 | convolution fusion | flops 331776000 | bytes 17408640 | tf_op jit(solution)/shard_map/sndp,dtspc->sntc/dot_general | solution.py:454
  431.0 8.4 fusion.20
  443.6 15.8 %convert_bitcast_fusion = bf16[16,2,20,40,20]{3,4,0,1,2:T(8,128)(2,1)} fusion(bf16[20,320,16,40]{1,3,2,0:T(8,128)(2,1)} %bitcast.167, pred[16,40]{1,0:T(8,128)(4,1)S(1)} %broadcast_in_dim.72, f32[20,20]{1,0:T(8,128)S(1)} %get-tuple-element.65, f32[276,2,20,320]{0,3,1,2:T(8,128)} %copy.30, f32[20,320,2,20,1]{3,1,4,2,0:T(8,128)} %fusion.6, ...), kind=kOutput, calls=%fused_computation.49 | convolution fusion | flops 333568000 | bytes 23989440 | tf_op jit(solution)/shard_map/sndp,sntc->dtspc/dot_general | solution.py:463
  459.4 8.6 %copy.54 = bf16[16,2,20,40,20]{4,3,0,1,2:T(8,128)(2,1)} copy(bf16[16,2,20,40,20]{3,4,0,1,2:T(8,128)(2,1)} %convert_bitcast_fusion) | data formatting | bytes 2048000
  468.0 7.9 pad.23.clone
  475.9 8.8 %reshape.416 = bf16[16,2,20,8,120]{4,3,0,1,2:T(8,128)(2,1)S(1)} reshape(bf16[16,2,20,48,20]{4,3,0,1,2:T(8,128)(2,1)} %pad.23.clone) | data formatting | bytes 2457600 | tf_op jit(solution)/shard_map/reshape | solution.py:491
  485.2 12.1 %fusion.36 = bf16[16,2,20,40,128]{4,3,0,1,2:T(8,128)(2,1)} fusion(bf16[20,320,16,40]{1,3,2,0:T(8,128)(2,1)} %bitcast.168, pred[16,40]{1,0:T(8,128)(4,1)S(1)} %broadcast_in_dim.72, f32[20,128]{1,0:T(8,128)S(1)} %get-tuple-element.67, f32[276,2,20,320]{0,3,1,2:T(8,128)} %copy.30, f32[20,320,2,128,1]{3,1,4,2,0:T(8,128)} %fusion.8, f32[20,320]{1,0:T(8,128)S(1)} %fusion.63), kind=kOutput, calls=%fused_computation.47 | convolution fusion | flops 2112716800 | bytes 29527680 | tf_op jit(solution)/shard_map/sndp,sntc->dtspc/dot_general | solution.py:463
  504.4 19.1 %all-to-all-done.4 = bf16[640,40,128]{2,1,0:T(8,128)(2,1)} async-done(((bf16[640,40,128]{2,1,0:T(8,128)(2,1)}), bf16[640,40,128]{2,1,0:T(8,128)(2,1)}, u32[]{:S(2)}, u32[]{:S(2)}) %all-to-all-start.4) | async-done | bytes 6553632 | tf_op jit(solution)/shard_map/all_to_all | solution.py:427
  532.0 113.1 %all-to-all-done.3 = bf16[640,32,128]{2,1,0:T(8,128)(2,1)} async-done(((bf16[640,32,128]{2,1,0:T(8,128)(2,1)}), bf16[640,32,128]{2,1,0:T(8,128)(2,1)}, u32[]{:S(2)}, u32[]{:S(2)}) %all-to-all-start.3) | async-done | bytes 5242912 | tf_op jit(solution)/shard_map/all_to_all | solution.py:427
  651.2 15.2 %pad_maximum_fusion = f32[276,2,20,320]{0,3,1,2:T(8,128)} fusion(f32[20,2,20,320]{0,3,1,2:T(8,128)} %get-tuple-element.53, f32[128,2,20,320]{0,3,1,2:T(8,128)} %get-tuple-element.54, f32[128,2,20,320]{0,3,1,2:T(8,128)} %get-tuple-element.55), kind=kLoop, calls=%fused_computation.2 | loop fusion | flops 7065600 | bytes 28262400 | tf_op jit(solution)/shard_map/concatenate | solution.py:499
  666.3 25.6 %copy.29 = f32[276,2,20,320]{3,1,2,0:T(2,128)} copy(f32[276,2,20,320]{0,3,1,2:T(8,128)} %pad_maximum_fusion) | data formatting | bytes 28262400 | tf_op jit(solution)/shard_map/concatenate | solution.py:499
  691.9 66.8 %adjoint_dft.3.refs_2_ = bf16[276,40,1408]{2,1,0:T(8,128)(2,1)} custom-call(s32[40]{0:T(128)} %copy-done.3, f32[40,16,768]{2,1,0:T(8,128)} %pad.22.ph_ref, bf16[16,2,20,40,128]{4,3,2,1,0:T(8,128)(2,1)} %bitcast.37.refs_0_), custom_call_target="tpu_custom_call" | custom-call | flops 5536481280 | bytes 20971520 | tf_op jit(solution)/shard_map/adjoint_dft/pallas_call | solution.py:349
  760.1 46.2 %adjoint_dft.4 = (bf16[276,40,1408]{2,1,0:T(8,128)(2,1)}, bf16[32,40,1408]{2,1,0:T(8,128)(2,1)}) custom-call(s32[40]{0:T(128)} %copy-done.3, f32[40,16,768]{2,1,0:T(8,128)} %pad.22.ph_ref, bf16[16,2,20,32,128]{4,3,2,1,0:T(8,128)(2,1)} %bitcast.32.refs_0_.refs_1_, ...), custom_call_target="tpu_custom_call", output_to_operand_aliasing={{0}: (4, {})} | custom-call | flops 3321888768 | bytes 12582912 | tf_op jit(solution)/shard_map/adjoint_dft/pallas_call | solution.py:349
  811.6 33.6 %adjoint_dft.5 = (bf16[276,40,1408]{2,1,0:T(8,128)(2,1)}, bf16[32,40,1408]{2,1,0:T(8,128)(2,1)}) custom-call(s32[40]{0:T(128)} %copy-done.3, f32[40,16,768]{2,1,0:T(8,128)} %pad.22.ph_ref, bf16[16,2,20,16,128]{4,3,2,1,0:T(8,128)(2,1)} %bitcast.160, ...), custom_call_target="tpu_custom_call", output_to_operand_aliasing={{0}: (4, {}), {1}: (5, {})} | custom-call | flops 2214592512 | bytes 8388608 | tf_op jit(solution)/shard_map/adjoint_dft/pallas_call | solution.py:349
  (60 shorter events, 53.7 us)
Async XLA Ops:
  0.6 0.8 copy-start
  2.9 5.4 copy-start.3
  33.7 66.3 %all-to-all-start = ((bf16[640,16,128]{2,1,0:T(8,128)(2,1)}), bf16[640,16,128]{2,1,0:T(8,128)(2,1)S(1)}, u32[]{:S(2)}, u32[]{:S(2)}) async-start(bf16[640,16,128]{2,1,0:T(8,128)(2,1)} %bitcast.161), calls=%async_computation | async-start | bytes 5242880 | tf_op jit(solution)/shard_map/all_to_all | solution.py:427
  100.0 91.8 %all-to-all-start.1 = ((bf16[640,24,128]{2,1,0:T(8,128)(2,1)}), bf16[640,24,128]{2,1,0:T(8,128)(2,1)}, u32[]{:S(2)}, u32[]{:S(2)}) async-start(bf16[640,24,128]{2,1,0:T(8,128)(2,1)} %bitcast.159), calls=%async_computation.1 | async-start | bytes 7864320 | tf_op jit(solution)/shard_map/all_to_all | solution.py:427
  191.8 8.1 copy-start.4
  191.8 8.2 copy-start.5
  191.8 183.7 %all-to-all-start.2 = ((bf16[640,48,128]{2,1,0:T(8,128)(2,1)}), bf16[640,48,128]{2,1,0:T(8,128)(2,1)}, u32[]{:S(2)}, u32[]{:S(2)}) async-start(bf16[640,48,128]{2,1,0:T(8,128)(2,1)} %bitcast.154), calls=%async_computation.2 | async-start | bytes 15728640 | tf_op jit(solution)/shard_map/all_to_all | solution.py:427
  375.5 148.0 %all-to-all-start.4 = ((bf16[640,40,128]{2,1,0:T(8,128)(2,1)}), bf16[640,40,128]{2,1,0:T(8,128)(2,1)}, u32[]{:S(2)}, u32[]{:S(2)}) async-start(bf16[640,40,128]{2,1,0:T(8,128)(2,1)} %bitcast.155), calls=%async_computation.4 | async-start | bytes 13107200 | tf_op jit(solution)/shard_map/all_to_all | solution.py:427
  497.3 2.2 slice-start
  523.5 6.3 slice-start.1
  523.5 121.6 %all-to-all-start.3 = ((bf16[640,32,128]{2,1,0:T(8,128)(2,1)}), bf16[640,32,128]{2,1,0:T(8,128)(2,1)}, u32[]{:S(2)}, u32[]{:S(2)}) async-start(bf16[640,32,128]{2,1,0:T(8,128)(2,1)} %bitcast.156), calls=%async_computation.3 | async-start | bytes 10485760 | tf_op jit(solution)/shard_map/all_to_all | solution.py:427
  645.1 164.9 %all-to-all-start.5 = ((bf16[640,16,128]{2,1,0:T(8,128)(2,1)}), bf16[640,16,128]{2,1,0:T(8,128)(2,1)S(1)}, u32[]{:S(2)}, u32[]{:S(2)}) async-start(bf16[640,16,128]{2,1,0:T(8,128)(2,1)} %bitcast.162), calls=%async_computation.5 | async-start | bytes 5242880 | tf_op jit(solution)/shard_map/all_to_all | solution.py:427
  810.1 1.5 copy-start.2
  811.6 36.7 %copy-start.1 = (s32[640]{0:T(1024)S(1)}, s32[640]{0:T(1024)}, u32[]{:S(2)}) copy-start(s32[640]{0:T(1024)} %param.11) | copy-start | bytes 7684

commit v4 on v3

--- a/solution.py
+++ b/solution.py
@@ -11,6 +11,8 @@
 
 STEPS = 2
 KB = 256
+BASE = 128
+BITS = 7
 GROUP = 8
 LANES = 128
 SPLIT = 3
@@ -21,7 +23,7 @@
 
 
 def phasor_rows(lengths, wave_ids, block_count, wave_pad):
-    exponents = [1 << bit for bit in range(8)] + [KB * block for block in range(block_count)]
+    exponents = [1 << bit for bit in range(BITS)] + [BASE * at for at in range(block_count * (KB // BASE))]
     exponents = jnp.asarray(exponents, dtype=jnp.int32)
     length = lengths[:, None, None]
     length_f = length.astype(jnp.float32)
@@ -68,7 +70,7 @@
     base_ref[0:8, :wave_pad] = cos_v
     base_ref[0:8, wave_pad:] = sin_v
     size, bit = 8, 3
-    while size < KB:
+    while size < BASE:
         cos_b = ph_ref[slot, bit : bit + 1, :wave_pad]
         sin_b = ph_ref[slot, bit : bit + 1, wave_pad:]
         for start in range(0, size, 32):
@@ -82,15 +84,16 @@
 
 
 def table_block(ph_ref, base_ref, table_ref, slot, block, wave_pad):
-    turn = ph_ref[slot, pl.ds(8 + block, 1), :]
-    cos_b, sin_b = turn[:, :wave_pad], turn[:, wave_pad:]
-    for start in range(0, KB, 32):
-        stop = start + 32
-        cos_v, sin_v = rotate(
-            base_ref[start:stop, :wave_pad], base_ref[start:stop, wave_pad:], cos_b, sin_b
-        )
-        table_ref[start:stop, :wave_pad] = cos_v.astype(jnp.bfloat16)
-        table_ref[start:stop, wave_pad:] = sin_v.astype(jnp.bfloat16)
+    for half in range(KB // BASE):
+        turn = ph_ref[slot, pl.ds(BITS + block * (KB // BASE) + half, 1), :]
+        cos_b, sin_b = turn[:, :wave_pad], turn[:, wave_pad:]
+        for start in range(0, BASE, 32):
+            cos_v, sin_v = rotate(
+                base_ref[start : start + 32, :wave_pad], base_ref[start : start + 32, wave_pad:], cos_b, sin_b
+            )
+            rows = slice(half * BASE + start, half * BASE + start + 32)
+            table_ref[rows, :wave_pad] = cos_v.astype(jnp.bfloat16)
+            table_ref[rows, wave_pad:] = sin_v.astype(jnp.bfloat16)
 
 
 def forward_kernel(
@@ -193,7 +196,7 @@
     ]
     operands = [lengths, phasors, grid]
     scratch = [
-        pltpu.VMEM((KB, 2 * wave_pad), jnp.float32),
+        pltpu.VMEM((BASE, 2 * wave_pad), jnp.float32),
         pltpu.VMEM((KB, 2 * wave_pad), jnp.bfloat16),
         pltpu.VMEM((wide_lanes, LANES * GROUP, LANES), jnp.float32),
         pltpu.VMEM((LANES + rest_cols, 2 * wave_pad), jnp.float32),
@@ -325,7 +328,7 @@
     out_specs = [pl.BlockSpec((LANES, GROUP, segment), lambda g, n: (index, first + g, 0))]
     out_shapes = [jax.ShapeDtypeStruct(out_shape, jnp.bfloat16)]
     scratch = [
-        pltpu.VMEM((KB, 2 * wave_pad), jnp.float32),
+        pltpu.VMEM((BASE, 2 * wave_pad), jnp.float32),
         pltpu.VMEM((KB, 2 * wave_pad), jnp.bfloat16),
         pltpu.VMEM((LANES + rest_cols, 2 * wave_pad), jnp.bfloat16),
         pltpu.VMEM((2 * wave_count * GROUP, LANES), jnp.float32),
@@ -402,7 +405,7 @@
     col_count = batch_size * chan_count
     wave_pad = round_up(wave_count, LANES)
     block_count = pl.cdiv(segment, KB)
-    scale_row = 8 + block_count
+    scale_row = BITS + block_count * (KB // BASE)
     lat_index = lax.axis_index("lat")
     my_cycles = lax.dynamic_slice_in_dim(cycle_ids, lat_index * cycle_dev, cycle_dev)
     lengths = jnp.take(cycle_len, my_cycles)

time: 865 us -> 862 us (level)
  Pallas kernels: 280 us -> 271 us
  transfers between devices with their start and end apart: 6 -> 6, of which waited for: 5 -> 5; matrix products, arithmetic and copies ran while one was open for 32% -> 32% of each run, Pallas kernels for 26% -> 25%
where the time goes in v4:
time: 862 us; the launch traced here: 846 us
  Pallas kernels  271 us (31%)
  waiting for transfers between devices  240 us (28%)
  local copies, waits for them, and re-layouts  157 us (18%)
  matrix products  75 us (9%)
  other arithmetic  50.9 us (6%)
  starting transfers between devices  40.1 us (5%)
  between operations  9.89 us (1%)
    all_to_all x6, waiting for transfers between devices, exchange(): lax.all_to_all(flat, 'lat', split_axis=0, concat_axis=0, tiled=True)  240 us
    pallas_call x3, Pallas kernels, adjoint_dft(): pl.pallas_call(functools.partial(adjoint_kernel, wave_count, wave_pad, sc...  143 us
    pallas_call x3, Pallas kernels, forward_dft(): pl.pallas_call(functools.partial(forward_kernel, wave_count, wave_pad, sc...  128 us
    optimization_barrier x2, local copies, waits for them, and re-layouts, device_program(): lax.optimization_barrier((part, lengths, legendre, target3))  41.4 us
    all_to_all x6, starting transfers between devices, exchange(): lax.all_to_all(flat, 'lat', split_axis=0, concat_axis=0, tiled=True)  40.1 us
    dot_general x3, matrix products, owner_pass(): jnp.einsum('sndp,sntc->dtspc', legendre_cols, grad_coeff, preferred_eleme...  39.8 us
    gather x2, local copies, waits for them, and re-layouts, device_program(): jnp.take(legendre, cycle_ids, axis=2)  35.4 us
    dot_general x3, matrix products, owner_pass(): jnp.einsum('sndp,dtspc->sntc', legendre_cols, gathered, preferred_element...  35.2 us
  transfers between devices with their start and end apart: 6, of which 5 were waited for; matrix products, arithmetic and copies ran while one was open for 32% of the time, Pallas kernels for 25%

profile of v4, /device:TPU:28, one launch (start us, length us, event | category | flops | bytes accessed | tf_op | source)
XLA Modules:
  0.0 846.2 jit_solution(13222972799911178387)
XLA Ops:
  9.6 24.5 %forward_dft.3 = bf16[16,2,20,16,128]{4,3,2,1,0:T(8,128)(2,1)} custom-call(s32[40]{0:T(128)} %copy-done.3, f32[40,24,768]{2,1,0:T(8,128)} %pad.22.ph_ref, bf16[276,40,1408]{2,1,0:T(8,128)(2,1)} %bitcast.148), custom_call_target="tpu_custom_call" | custom-call | flops 2214592512 | bytes 8388608 | tf_op jit(solution)/shard_map/forward_dft/pallas_call | solution.py:214
  34.1 8.1 all-to-all-start
  42.2 35.8 %forward_dft.4 = bf16[16,2,20,24,128]{4,3,2,1,0:T(8,128)(2,1)} custom-call(s32[40]{0:T(128)} %copy-done.3, f32[40,24,768]{2,1,0:T(8,128)} %pad.22.ph_ref, bf16[276,40,1408]{2,1,0:T(8,128)(2,1)} %bitcast.149), custom_call_target="tpu_custom_call" | custom-call | flops 3321888768 | bytes 12582912 | tf_op jit(solution)/shard_map/forward_dft/pallas_call | solution.py:214
  78.0 22.4 %all-to-all-done = bf16[640,16,128]{2,1,0:T(8,128)(2,1)S(1)} async-done(((bf16[640,16,128]{2,1,0:T(8,128)(2,1)}), bf16[640,16,128]{2,1,0:T(8,128)(2,1)S(1)}, u32[]{:S(2)}, u32[]{:S(2)}) %all-to-all-start) | async-done | bytes 2621472 | tf_op jit(solution)/shard_map/all_to_all | solution.py:430
  106.7 67.6 %forward_dft.5 = bf16[16,2,20,48,128]{4,3,2,1,0:T(8,128)(2,1)} custom-call(s32[40]{0:T(128)} %copy-done.3, f32[40,24,768]{2,1,0:T(8,128)} %pad.22.ph_ref, bf16[276,40,1408]{2,1,0:T(8,128)(2,1)} %bitcast.150, bf16[276,40,1408]{2,1,0:T(8,128)(2,1)} %bitcast.151), custom_call_target="tpu_custom_call" | custom-call | flops 5536481280 | bytes 20971520 | tf_op jit(solution)/shard_map/forward_dft/pallas_call | solution.py:214
  174.3 17.9 %all-to-all-done.1 = bf16[640,24,128]{2,1,0:T(8,128)(2,1)} async-done(((bf16[640,24,128]{2,1,0:T(8,128)(2,1)}), bf16[640,24,128]{2,1,0:T(8,128)(2,1)}, u32[]{:S(2)}, u32[]{:S(2)}) %all-to-all-start.1) | async-done | bytes 3932192 | tf_op jit(solution)/shard_map/all_to_all | solution.py:430
  192.2 7.1 all-to-all-start.2
  200.2 15.0 %copy.22 = bf16[20,320,640]{1,0,2:T(8,128)(2,1)} copy(bf16[20,320,640]{2,1,0:T(8,128)(2,1)} %param.13) | data formatting | bytes 16384000 | tf_op jit(solution)/shard_map/optimization_barrier | solution.py:449
  215.2 25.5 %gather_fusion.1 = bf16[640,20,320]{2,1,0:T(8,128)(2,1)} fusion(bf16[20,320,640]{1,0,2:T(8,128)(2,1)} %copy.22, s32[1024]{0:T(1024)S(1)} %pad_clamp_fusion), kind=kCustom, calls=%fused_computation.1 | custom fusion | bytes 16386560 | tf_op jit(solution)/shard_map/jit(_take)/gather | solution.py:452
  240.7 9.9 %copy.23 = bf16[20,320,640]{1,2,0:T(8,128)(2,1)} copy(bf16[20,320,640]{1,0,2:T(8,128)(2,1)} %bitcast.153) | data formatting | bytes 16384000 | tf_op jit(solution)/shard_map/jit(_take)/gather | solution.py:452
  250.6 26.5 %copy.30 = f32[276,2,20,320]{0,3,1,2:T(8,128)} copy(f32[276,2,20,320]{3,1,2,0:T(2,128)} %bitcast.157) | data formatting | bytes 28262400 | tf_op jit(solution)/shard_map/optimization_barrier | solution.py:449
  278.0 11.4 %fusion.10 = f32[20,320,2,128,1]{3,1,4,2,0:T(8,128)} fusion(bf16[20,320,16,40]{1,3,2,0:T(8,128)(2,1)} %bitcast.163, pred[16,40]{1,0:T(8,128)(4,1)S(1)} %broadcast_in_dim.72, bf16[16,2,20,24,128]{4,3,2,1,0:T(8,128)(2,1)} %bitcast.9, bf16[16,2,20,16,128]{4,3,2,1,0:T(8,128)(2,1)S(1)} %bitcast.169), kind=kOutput, calls=%fused_computation.13 | convolution fusion | flops 2114355200 | bytes 21299840 | tf_op jit(solution)/shard_map/sndp,dtspc->sntc/dot_general | solution.py:457
  289.4 12.0 %fusion.33 = bf16[16,2,20,40,128]{4,3,0,1,2:T(8,128)(2,1)} fusion(bf16[20,320,16,40]{1,3,2,0:T(8,128)(2,1)} %bitcast.164, pred[16,40]{1,0:T(8,128)(4,1)S(1)} %broadcast_in_dim.72, f32[20,128]{1,0:T(8,128)S(1)} %get-tuple-element.60, f32[276,2,20,320]{0,3,1,2:T(8,128)} %copy.30, f32[20,320,2,128,1]{3,1,4,2,0:T(8,128)} %fusion.10, f32[20,320]{1,0:T(8,128)S(1)} %fusion.63), kind=kOutput, calls=%fused_computation.46 | convolution fusion | flops 2112716800 | bytes 29527680 | tf_op jit(solution)/shard_map/sndp,sntc->dtspc/dot_general | solution.py:466
  301.4 7.3 copy.37
  308.7 66.9 %all-to-all-done.2 = bf16[640,48,128]{2,1,0:T(8,128)(2,1)} async-done(((bf16[640,48,128]{2,1,0:T(8,128)(2,1)}), bf16[640,48,128]{2,1,0:T(8,128)(2,1)}, u32[]{:S(2)}, u32[]{:S(2)}) %all-to-all-start.2) | async-done | bytes 7864352 | tf_op jit(solution)/shard_map/all_to_all | solution.py:430
  383.5 7.0 reshape.380
  390.5 11.9 %fusion.8 = f32[20,320,2,128,1]{3,1,4,2,0:T(8,128)} fusion(bf16[20,320,16,40]{1,3,2,0:T(8,128)(2,1)} %bitcast.165, pred[16,40]{1,0:T(8,128)(4,1)S(1)} %broadcast_in_dim.72, bf16[16,2,20,48,128]{4,3,2,1,0:T(8,128)(2,1)} %bitcast.15), kind=kOutput, calls=%fused_computation.11 | convolution fusion | flops 2101248000 | bytes 22938240 | tf_op jit(solution)/shard_map/sndp,dtspc->sntc/dot_general | solution.py:457
  402.4 15.4 %fusion.19 = (f32[]{:T(128)}, f32[]{:T(128)}, f32[128,2,20,320]{0,3,1,2:T(8,128)}, f32[128,2,20,320]{0,3,1,2:T(8,128)}) fusion(f32[20,128]{1,0:T(8,128)S(1)} %get-tuple-element.66, f32[276,2,20,320]{0,3,1,2:T(8,128)} %copy.30, f32[20,320]{1,0:T(8,128)S(1)} %fusion.63, f32[20,320,2,128,1]{3,1,4,2,0:T(8,128)} %fusion.8, f32[20,320,2,128,1]{3,1,4,2,0:T(8,128)} %fusion.10, ...), kind=kLoop, calls=%fused_computation.22 | loop fusion | flops 19660800 | bytes 39367688 | tf_op jit(solution)/shard_map/reduce_sum | solution.py:464
  419.2 11.9 %fusion.6 = f32[20,320,2,20,1]{3,1,4,2,0:T(8,128)} fusion(bf16[20,320,16,40]{1,3,2,0:T(8,128)(2,1)} %bitcast.166, pred[16,40]{1,0:T(8,128)(4,1)S(1)} %broadcast_in_dim.72, bf16[16,2,20,48,20]{4,3,2,1,0:T(8,128)(2,1)} %reshape.380), kind=kOutput, calls=%fused_computation.9 | convolution fusion | flops 331776000 | bytes 17408640 | tf_op jit(solution)/shard_map/sndp,dtspc->sntc/dot_general | solution.py:457
  431.1 8.4 fusion.20
  443.7 15.6 %convert_bitcast_fusion = bf16[16,2,20,40,20]{3,4,0,1,2:T(8,128)(2,1)} fusion(bf16[20,320,16,40]{1,3,2,0:T(8,128)(2,1)} %bitcast.167, pred[16,40]{1,0:T(8,128)(4,1)S(1)} %broadcast_in_dim.72, f32[20,20]{1,0:T(8,128)S(1)} %get-tuple-element.65, f32[276,2,20,320]{0,3,1,2:T(8,128)} %copy.30, f32[20,320,2,20,1]{3,1,4,2,0:T(8,128)} %fusion.6, ...), kind=kOutput, calls=%fused_computation.51 | convolution fusion | flops 333568000 | bytes 23989440 | tf_op jit(solution)/shard_map/sndp,sntc->dtspc/dot_general | solution.py:466
  459.3 8.6 %copy.54 = bf16[16,2,20,40,20]{4,3,0,1,2:T(8,128)(2,1)} copy(bf16[16,2,20,40,20]{3,4,0,1,2:T(8,128)(2,1)} %convert_bitcast_fusion) | data formatting | bytes 2048000
  467.9 7.9 pad.23.clone
  475.8 8.8 %reshape.416 = bf16[16,2,20,8,120]{4,3,0,1,2:T(8,128)(2,1)S(1)} reshape(bf16[16,2,20,48,20]{4,3,0,1,2:T(8,128)(2,1)} %pad.23.clone) | data formatting | bytes 2457600 | tf_op jit(solution)/shard_map/reshape | solution.py:494
  485.1 12.2 %fusion.36 = bf16[16,2,20,40,128]{4,3,0,1,2:T(8,128)(2,1)} fusion(bf16[20,320,16,40]{1,3,2,0:T(8,128)(2,1)} %bitcast.168, pred[16,40]{1,0:T(8,128)(4,1)S(1)} %broadcast_in_dim.72, f32[20,128]{1,0:T(8,128)S(1)} %get-tuple-element.67, f32[276,2,20,320]{0,3,1,2:T(8,128)} %copy.30, f32[20,320,2,128,1]{3,1,4,2,0:T(8,128)} %fusion.8, f32[20,320]{1,0:T(8,128)S(1)} %fusion.63), kind=kOutput, calls=%fused_computation.47 | convolution fusion | flops 2112716800 | bytes 29527680 | tf_op jit(solution)/shard_map/sndp,sntc->dtspc/dot_general | solution.py:466
  504.4 19.2 %all-to-all-done.4 = bf16[640,40,128]{2,1,0:T(8,128)(2,1)} async-done(((bf16[640,40,128]{2,1,0:T(8,128)(2,1)}), bf16[640,40,128]{2,1,0:T(8,128)(2,1)}, u32[]{:S(2)}, u32[]{:S(2)}) %all-to-all-start.4) | async-done | bytes 6553632 | tf_op jit(solution)/shard_map/all_to_all | solution.py:430
  532.1 113.1 %all-to-all-done.3 = bf16[640,32,128]{2,1,0:T(8,128)(2,1)} async-done(((bf16[640,32,128]{2,1,0:T(8,128)(2,1)}), bf16[640,32,128]{2,1,0:T(8,128)(2,1)}, u32[]{:S(2)}, u32[]{:S(2)}) %all-to-all-start.3) | async-done | bytes 5242912 | tf_op jit(solution)/shard_map/all_to_all | solution.py:430
  651.3 15.2 %pad_maximum_fusion = f32[276,2,20,320]{0,3,1,2:T(8,128)} fusion(f32[20,2,20,320]{0,3,1,2:T(8,128)} %get-tuple-element.53, f32[128,2,20,320]{0,3,1,2:T(8,128)} %get-tuple-element.54, f32[128,2,20,320]{0,3,1,2:T(8,128)} %get-tuple-element.55), kind=kLoop, calls=%fused_computation.2 | loop fusion | flops 7065600 | bytes 28262400 | tf_op jit(solution)/shard_map/concatenate | solution.py:502
  666.4 25.6 %copy.29 = f32[276,2,20,320]{3,1,2,0:T(2,128)} copy(f32[276,2,20,320]{0,3,1,2:T(8,128)} %pad_maximum_fusion) | data formatting | bytes 28262400 | tf_op jit(solution)/shard_map/concatenate | solution.py:502
  692.0 64.8 %adjoint_dft.3.refs_2_ = bf16[276,40,1408]{2,1,0:T(8,128)(2,1)} custom-call(s32[40]{0:T(128)} %copy-done.3, f32[40,24,768]{2,1,0:T(8,128)} %pad.22.ph_ref, bf16[16,2,20,40,128]{4,3,2,1,0:T(8,128)(2,1)} %bitcast.37.refs_0_), custom_call_target="tpu_custom_call" | custom-call | flops 5536481280 | bytes 20971520 | tf_op jit(solution)/shard_map/adjoint_dft/pallas_call | solution.py:352
  758.2 45.1 %adjoint_dft.4 = (bf16[276,40,1408]{2,1,0:T(8,128)(2,1)}, bf16[32,40,1408]{2,1,0:T(8,128)(2,1)}) custom-call(s32[40]{0:T(128)} %copy-done.3, f32[40,24,768]{2,1,0:T(8,128)} %pad.22.ph_ref, bf16[16,2,20,32,128]{4,3,2,1,0:T(8,128)(2,1)} %bitcast.32.refs_0_.refs_1_, ...), custom_call_target="tpu_custom_call", output_to_operand_aliasing={{0}: (4, {})} | custom-call | flops 3321888768 | bytes 12582912 | tf_op jit(solution)/shard_map/adjoint_dft/pallas_call | solution.py:352
  808.6 32.9 %adjoint_dft.5 = (bf16[276,40,1408]{2,1,0:T(8,128)(2,1)}, bf16[32,40,1408]{2,1,0:T(8,128)(2,1)}) custom-call(s32[40]{0:T(128)} %copy-done.3, f32[40,24,768]{2,1,0:T(8,128)} %pad.22.ph_ref, bf16[16,2,20,16,128]{4,3,2,1,0:T(8,128)(2,1)} %bitcast.160, ...), custom_call_target="tpu_custom_call", output_to_operand_aliasing={{0}: (4, {}), {1}: (5, {})} | custom-call | flops 2214592512 | bytes 8388608 | tf_op jit(solution)/shard_map/adjoint_dft/pallas_call | solution.py:352
  (60 shorter events, 54.9 us)
Async XLA Ops:
  0.6 0.8 copy-start
  2.9 6.6 copy-start.3
  34.1 66.3 %all-to-all-start = ((bf16[640,16,128]{2,1,0:T(8,128)(2,1)}), bf16[640,16,128]{2,1,0:T(8,128)(2,1)S(1)}, u32[]{:S(2)}, u32[]{:S(2)}) async-start(bf16[640,16,128]{2,1,0:T(8,128)(2,1)} %bitcast.161), calls=%async_computation | async-start | bytes 5242880 | tf_op jit(solution)/shard_map/all_to_all | solution.py:430
  100.4 91.8 %all-to-all-start.1 = ((bf16[640,24,128]{2,1,0:T(8,128)(2,1)}), bf16[640,24,128]{2,1,0:T(8,128)(2,1)}, u32[]{:S(2)}, u32[]{:S(2)}) async-start(bf16[640,24,128]{2,1,0:T(8,128)(2,1)} %bitcast.159), calls=%async_computation.1 | async-start | bytes 7864320 | tf_op jit(solution)/shard_map/all_to_all | solution.py:430
  192.2 7.8 copy-start.4
  192.2 7.9 copy-start.5
  192.2 183.4 %all-to-all-start.2 = ((bf16[640,48,128]{2,1,0:T(8,128)(2,1)}), bf16[640,48,128]{2,1,0:T(8,128)(2,1)}, u32[]{:S(2)}, u32[]{:S(2)}) async-start(bf16[640,48,128]{2,1,0:T(8,128)(2,1)} %bitcast.154), calls=%async_computation.2 | async-start | bytes 15728640 | tf_op jit(solution)/shard_map/all_to_all | solution.py:430
  375.6 148.0 %all-to-all-start.4 = ((bf16[640,40,128]{2,1,0:T(8,128)(2,1)}), bf16[640,40,128]{2,1,0:T(8,128)(2,1)}, u32[]{:S(2)}, u32[]{:S(2)}) async-start(bf16[640,40,128]{2,1,0:T(8,128)(2,1)} %bitcast.155), calls=%async_computation.4 | async-start | bytes 13107200 | tf_op jit(solution)/shard_map/all_to_all | solution.py:430
  497.3 2.2 slice-start
  523.6 6.3 slice-start.1
  523.6 121.6 %all-to-all-start.3 = ((bf16[640,32,128]{2,1,0:T(8,128)(2,1)}), bf16[640,32,128]{2,1,0:T(8,128)(2,1)}, u32[]{:S(2)}, u32[]{:S(2)}) async-start(bf16[640,32,128]{2,1,0:T(8,128)(2,1)} %bitcast.156), calls=%async_computation.3 | async-start | bytes 10485760 | tf_op jit(solution)/shard_map/all_to_all | solution.py:430
  645.2 161.9 %all-to-all-start.5 = ((bf16[640,16,128]{2,1,0:T(8,128)(2,1)}), bf16[640,16,128]{2,1,0:T(8,128)(2,1)S(1)}, u32[]{:S(2)}, u32[]{:S(2)}) async-start(bf16[640,16,128]{2,1,0:T(8,128)(2,1)} %bitcast.162), calls=%async_computation.5 | async-start | bytes 5242880 | tf_op jit(solution)/shard_map/all_to_all | solution.py:430
  807.1 1.5 copy-start.2
  808.6 36.0 %copy-start.1 = (s32[640]{0:T(1024)S(1)}, s32[640]{0:T(1024)}, u32[]{:S(2)}) copy-start(s32[640]{0:T(1024)} %param.11) | copy-start | bytes 7684
